TPU v7x, 512 devices: a whole 4x4x16 slice. The times are simulated.
512 devices in a mesh: grp: 32 (over z_lo, y, core), fsdp: 16 (over x, z_hi).
Axes of the slice: x: 4, y: 4, z: 16 (z_hi: 4, z_lo: 4; z = z_hi * 4 + z_lo), core: 2. Of those that a mesh axis runs over, the one named last changes fastest.
Arguments:
- layer_inputs: bfloat16 [32, 8192, 2048], P('grp', 'fsdp'), may hold values from -6 to 6
- key_cotangent: bfloat16 [32, 8192, 768], P('grp', 'fsdp'), may hold values from -0.099609375 to 0.099609375
- key_weights: bfloat16 [2048, 768], P('fsdp'), may hold values from -0.125 to 0.125
- outer_momentum: float32 [2048, 768], P('fsdp'), may hold values from -0.02 to 0.02
- state_codes: int32 [32, 2048, 768], P('grp', 'fsdp'), may hold values from 0 to 255
- first_row_max: float32 [32, 2048], P('grp', 'fsdp'), may hold values from 0.1 to 2
- first_col_max: float32 [32, 768], P('grp'), may hold values from 0.1 to 2
- second_row_max: float32 [32, 2048], P('grp', 'fsdp'), may hold values from 0.1 to 4
- second_col_max: float32 [32, 768], P('grp'), may hold values from 0.1 to 4
Outputs:
- new_weights: float32 [2048, 768], P('fsdp')
- new_momentum: float32 [2048, 768], P('fsdp')
- first_state: bfloat16 [32, 2048, 768], P('grp', 'fsdp')
- second_state: bfloat16 [32, 2048, 768], P('grp', 'fsdp')
- new_first_row_max: float32 [32, 2048], P('grp', 'fsdp')
- new_first_col_max: float32 [32, 768], P('grp')
- new_second_row_max: float32 [32, 2048], P('grp', 'fsdp')
- new_second_col_max: float32 [32, 768], P('grp')
- next_keys: bfloat16 [32, 8192, 768], P('grp', 'fsdp')
All inputs are finite; a program needn't handle non-finite values. Where the computation divides by a largest or mean magnitude, that divisor is 1e-20 or more.
Results may differ from a plain program's by a relative error of at most 0.018.
Values may be sent and summed in bfloat16 or wider, within the bound.
A program may use at most 64 MiB of HBM per device.

v0:
```python
import jax
import jax.numpy as jnp
from jax import lax
from jax.sharding import Mesh
from jax.sharding import PartitionSpec as P

FSDP = ("fsdp_0", "fsdp_1")


beta_one = 0.9
beta_two = 0.95
bias_one = 1.0 - 0.9**10
bias_two = 1.0 - 0.95**10
adam_eps = 1e-08
inner_rate = 0.01
weight_decay = 0.1
outer_rate = 0.7
outer_beta = 0.9
stat_eps = 1e-06


def own_rows(terms, axes):
    subtotal = terms.astype(jnp.bfloat16)
    for axis in axes:
        subtotal = lax.psum_scatter(subtotal, axis, scatter_dimension=0, tiled=True)
    return subtotal.astype(jnp.float32)


def copy_for_each(shard, axis):
    copies = jnp.broadcast_to(shard, (lax.axis_size(axis), *shard.shape))
    return lax.all_to_all(copies, axis, split_axis=0, concat_axis=0, tiled=True)


def of_everyone(shard, axis):
    everything = copy_for_each(shard, axis)
    return jnp.max(everything, axis=0)


def in_one(arrays, axis):
    ends = [0]
    for a in arrays:
        ends.append(ends[-1] + a.size)
    subtotal = of_everyone(jnp.concatenate([a.ravel() for a in arrays]), axis)
    return tuple((subtotal[b:e].reshape(a.shape) for a, b, e in zip(arrays, ends, ends[1:])))


def in_blocks(shard, dim, size):
    lengths = shard.shape
    tiles = shard.reshape(*lengths[:dim], size, lengths[dim] // size, *lengths[dim + 1 :])
    return jnp.moveaxis(tiles, dim, 0)


def sum_at_owner(shard, axis, dim):
    tiles = in_blocks(shard, dim, lax.axis_size(axis))
    arrived = lax.all_to_all(tiles, axis, split_axis=0, concat_axis=0, tiled=True)
    return arrived.sum(axis=0)


def side_by_side(arrays, axis, dim, along):
    widths = [a.shape[along] for a in arrays]
    both = jnp.concatenate(arrays, axis=along)
    filled = lax.all_gather(both, axis, axis=dim, tiled=True)
    return tuple(jnp.split(filled, [sum(widths[:k]) for k in range(1, len(widths))], axis=along))


def local(
    layer_inputs,
    key_cotangent,
    key_weights,
    outer_momentum,
    state_codes,
    first_row_max,
    first_col_max,
    second_row_max,
    second_col_max,
):
    tokens = layer_inputs[0]
    cotangent = key_cotangent[0]
    columns = tokens
    gradient = own_rows(
        lax.dot_general(
            columns, cotangent, (((0,), (0,)), ((), ())), preferred_element_type=jnp.float32
        ),
        FSDP,
    )
    packed_codes = state_codes[0]
    first_code = (packed_codes // 16).astype(jnp.float32)
    second_code = (packed_codes % 16).astype(jnp.float32)
    first_old = (
        jnp.minimum(first_row_max[0][:, None], first_col_max[0][None, :]) * (first_code - 7.5) / 7.5
    )
    second_old = (
        jnp.minimum(second_row_max[0][:, None], second_col_max[0][None, :])
        * ((second_code + 1.0) / 16.0) ** 2
    )
    first_new = beta_one * first_old + (1.0 - beta_one) * gradient
    second_new = beta_two * second_old + (1.0 - beta_two) * gradient * gradient
    weights_float = key_weights.astype(jnp.float32)
    update = first_new / bias_one / (jnp.sqrt(second_new / bias_two) + adam_eps)
    pseudo_grad = inner_rate * (update + weight_decay * weights_float)
    first_rmax = jnp.max(jnp.abs(first_new), axis=1) + stat_eps
    second_rmax = jnp.max(second_new, axis=1) + stat_eps
    first_local = jnp.max(jnp.abs(first_new), axis=0)
    second_local = jnp.max(second_new, axis=0)
    first_cmax, second_cmax = in_one((first_local, second_local), FSDP)
    first_cmax = first_cmax + stat_eps
    second_cmax = second_cmax + stat_eps
    first_state = (first_new / jnp.minimum(first_rmax[:, None], first_cmax[None, :])).astype(
        jnp.bfloat16
    )
    second_state = (second_new / jnp.minimum(second_rmax[:, None], second_cmax[None, :])).astype(
        jnp.bfloat16
    )
    group_count = lax.axis_size("grp")
    portion = sum_at_owner(pseudo_grad, "grp", 0)
    count = portion.shape[0]
    first_row = lax.axis_index("grp") * count
    old_part = lax.dynamic_slice_in_dim(outer_momentum, first_row, count, 0)
    averaged_part = portion / group_count
    momentum_part = outer_beta * old_part + averaged_part
    averaged, momentum = side_by_side((averaged_part, momentum_part), "grp", 0, 1)
    new_weights = weights_float - outer_rate * (averaged + outer_beta * momentum)
    weights_half = new_weights.astype(jnp.bfloat16)
    columns = tokens
    next_keys = jnp.dot(
        columns,
        lax.all_gather(weights_half, FSDP, axis=0, tiled=True),
        preferred_element_type=jnp.float32,
    )
    return (
        new_weights,
        momentum,
        first_state[None],
        second_state[None],
        first_rmax[None],
        first_cmax[None],
        second_rmax[None],
        second_cmax[None],
        next_keys.astype(jnp.bfloat16)[None],
    )


def solution(mesh):
    finer = Mesh(mesh.devices.reshape(mesh.shape["grp"], 4, 4), ("grp", "fsdp_0", "fsdp_1"))
    in_specs = (
        P("grp", FSDP, None),
        P("grp", FSDP, None),
        P(FSDP, None),
        P(FSDP, None),
        P("grp", FSDP, None),
        P("grp", FSDP),
        P("grp", None),
        P("grp", FSDP),
        P("grp", None),
    )
    out_specs = (
        P(FSDP, None),
        P(FSDP, None),
        P("grp", FSDP, None),
        P("grp", FSDP, None),
        P("grp", FSDP),
        P("grp", None),
        P("grp", FSDP),
        P("grp", None),
        P("grp", FSDP, None),
    )
    return jax.shard_map(local, mesh=finer, in_specs=in_specs, out_specs=out_specs, check_vma=False)
```

profile of v0, /device:TPU:1, one launch (start us, length us, event | category | flops | bytes accessed | tf_op | source)
XLA Modules:
  0.0 325.5 jit_solution(8753981273435014339)
XLA Ops:
  7.2 1.5 copy-done
  8.8 4.6 %convolution_convert_fusion = bf16[2048,768]{1,0:T(8,128)(2,1)} fusion(bf16[1,512,2048]{2,1,0:T(8,128)(2,1)S(1)} %copy-done, bf16[1,512,768]{2,1,0:T(8,128)(2,1)} %param.10), kind=kOutput, calls=%fused_computation | convolution fusion | flops 1612185600 | bytes 6029312 | tf_op jit(solution)/shard_map/dot_general | solution.py:81
  13.5 51.2 %reduce-scatter.3.cloned.1.call-done = bf16[512,768]{1,0:T(8,128)(2,1)} async-done(((bf16[2048,768]{1,0:T(8,128)(2,1)}), bf16[512,768]{1,0:T(8,128)(2,1)}) %reduce-scatter.3.cloned.1.call-update) | async-done | bytes 786448 | tf_op jit(solution)/shard_map/reduce_scatter | solution.py:25
  64.9 54.8 %reduce-scatter.5.cloned.1.call-done = bf16[128,768]{1,0:T(8,128)(2,1)} async-done(((bf16[512,768]{1,0:T(8,128)(2,1)}), bf16[128,768]{1,0:T(8,128)(2,1)}) %reduce-scatter.5.cloned.1.call-update) | async-done | bytes 196624 | tf_op jit(solution)/shard_map/reduce_scatter | solution.py:25
  119.7 1.6 abs_reduce_fusion.1
  121.3 0.7 broadcast_in_dim.24
  122.0 7.3 %all-to-all-start.1 = ((f32[16,1,1536]{2,1,0:T(1,128)}), f32[16,1,1536]{2,1,0:T(1,128)S(1)}, u32[]{:S(2)}, u32[]{:S(2)}) async-start(f32[16,1,1536]{2,1,0:T(1,128)} %broadcast_in_dim.24), calls=%async_computation.3 | async-start | bytes 196608 | tf_op jit(solution)/shard_map/all_to_all | solution.py:31
  129.3 0.5 fusion.30
  129.8 13.7 %all-to-all-done.1 = f32[16,1,1536]{2,1,0:T(1,128)S(1)} async-done(((f32[16,1,1536]{2,1,0:T(1,128)}), f32[16,1,1536]{2,1,0:T(1,128)S(1)}, u32[]{:S(2)}, u32[]{:S(2)}) %all-to-all-start.1) | async-done | bytes 98336 | tf_op jit(solution)/shard_map/all_to_all | solution.py:31
  143.6 0.1 reduce_max.48
  143.7 1.1 fusion.29
  144.7 0.9 reshape.53
  145.6 7.7 %all-to-all-start = ((f32[32,4,768]{2,1,0:T(4,128)}), f32[32,4,768]{2,1,0:T(4,128)S(1)}, u32[]{:S(2)}, u32[]{:S(2)}) async-start(f32[32,4,768]{2,1,0:T(4,128)} %reshape.53), calls=%async_computation.2 | async-start | bytes 786432 | tf_op jit(solution)/shard_map/all_to_all | solution.py:55
  153.4 13.7 %all-to-all-done = f32[32,4,768]{2,1,0:T(4,128)S(1)} async-done(((f32[32,4,768]{2,1,0:T(4,128)}), f32[32,4,768]{2,1,0:T(4,128)S(1)}, u32[]{:S(2)}, u32[]{:S(2)}) %all-to-all-start) | async-done | bytes 393248 | tf_op jit(solution)/shard_map/all_to_all | solution.py:55
  167.1 0.1 reduce_sum.9
  167.1 0.7 broadcast_multiply_fusion
  167.9 41.7 %all-gather = f32[32,4,1536]{2,1,0:T(4,128)S(1)} all-gather(f32[1,4,1536]{2,1,0:T(4,128)S(1)} %maximum_bitcast_fusion), channel_id=1, replica_groups=mesh['grp'=32,'fsdp_0'=4,'fsdp_1'=4] {'grp'}, dimensions={0}, use_global_device_ids=true | all-gather | bytes 811008 | tf_op jit(solution)/shard_map/all_gather | solution.py:62
  209.6 1.1 reshape.55
  210.8 2.1 fusion.33
  212.9 0.6 broadcast_in_dim.27
  213.5 0.6 broadcast_in_dim.28
  214.1 100.0 %all-gather.3.cloned.1.call-done = bf16[2048,768]{1,0:T(8,128)(2,1)} async-done(((bf16[128,768]{1,0:T(8,128)(2,1)}), bf16[2048,768]{1,0:T(8,128)(2,1)}) %all-gather.3.cloned.1.call-update) | async-done | bytes 3145744 | tf_op jit(solution)/shard_map/all_gather | solution.py:127
  314.1 3.7 %fusion.6 = bf16[1,512,768]{1,2,0:T(8,128)(2,1)S(1)} fusion(bf16[2048,768]{1,0:T(8,128)(2,1)} %all-gather.3.cloned.1.call-done, bf16[1,512,2048]{2,1,0:T(8,128)(2,1)S(1)} %copy-done), kind=kOutput, calls=%fused_computation.5 | convolution fusion | flops 1611005952 | bytes 6029312 | tf_op jit(solution)/shard_map/dot_general | solution.py:125
  317.8 1.2 copy.22
  (24 shorter events, 0.3 us)
Async XLA Ops:
  7.2 1.6 copy-start
  7.2 57.6 %reduce-scatter.3.cloned.1.call-start = ((), (), s32[]{:S(2)}) async-start(), calls=%async_computation.4 | async-start | bytes 3932160 | tf_op jit(solution)/shard_map/reduce_scatter | solution.py:25
  13.4 51.4 %copy-start.3 = (f32[1,768]{1,0:T(1,128)S(1)}, f32[1,768]{1,0:T(1,128)}, u32[]{:S(2)}) copy-start(f32[1,768]{1,0:T(1,128)} %param.15) | copy-start | bytes 9220
  13.4 51.4 %copy-start.4 = (f32[1,768]{1,0:T(1,128)S(1)}, f32[1,768]{1,0:T(1,128)}, u32[]{:S(2)}) copy-start(f32[1,768]{1,0:T(1,128)} %param.17) | copy-start | bytes 9220
  13.4 106.3 %copy-start.2 = (s32[1,128,768]{2,1,0:T(8,128)S(1)}, s32[1,128,768]{2,1,0:T(8,128)}, u32[]{:S(2)}) copy-start(s32[1,128,768]{2,1,0:T(8,128)} %param.13) | copy-start | bytes 1179652
  13.4 106.3 %copy-start.5 = (f32[1,128]{1,0:T(1,128)S(1)}, f32[1,128]{1,0:T(1,128)}, u32[]{:S(2)}) copy-start(f32[1,128]{1,0:T(1,128)} %param.14) | copy-start | bytes 1540
  13.4 106.3 %copy-start.6 = (f32[1,128]{1,0:T(1,128)S(1)}, f32[1,128]{1,0:T(1,128)}, u32[]{:S(2)}) copy-start(f32[1,128]{1,0:T(1,128)} %param.16) | copy-start | bytes 1540
  13.5 130.2 %copy-start.1 = (bf16[128,768]{1,0:T(8,128)(2,1)S(1)}, bf16[128,768]{1,0:T(8,128)(2,1)}, u32[]{:S(2)}) copy-start(bf16[128,768]{1,0:T(8,128)(2,1)} %param.11) | copy-start | bytes 589828
  13.5 106.2 %reduce-scatter.5.cloned.1.call-start = ((), (), s32[]{:S(2)}) async-start(), calls=%async_computation.5 | async-start | bytes 983040 | tf_op jit(solution)/shard_map/reduce_scatter | solution.py:25
  122.0 21.5 %all-to-all-start.1 = ((f32[16,1,1536]{2,1,0:T(1,128)}), f32[16,1,1536]{2,1,0:T(1,128)S(1)}, u32[]{:S(2)}, u32[]{:S(2)}) async-start(f32[16,1,1536]{2,1,0:T(1,128)} %broadcast_in_dim.24), calls=%async_computation.3 | async-start | bytes 196608 | tf_op jit(solution)/shard_map/all_to_all | solution.py:31
  145.6 21.5 %all-to-all-start = ((f32[32,4,768]{2,1,0:T(4,128)}), f32[32,4,768]{2,1,0:T(4,128)S(1)}, u32[]{:S(2)}, u32[]{:S(2)}) async-start(f32[32,4,768]{2,1,0:T(4,128)} %reshape.53), calls=%async_computation.2 | async-start | bytes 786432 | tf_op jit(solution)/shard_map/all_to_all | solution.py:55
  153.3 160.8 %all-gather.3.cloned.1.call-start = ((), (), s32[]{:S(2)}) async-start(), calls=%async_computation.6 | async-start | bytes 3342336 | tf_op jit(solution)/shard_map/all_gather | solution.py:127
Sparse Core Ops, SparseCore 0:
  13.6 51.1 reduce-scatter.2
  67.6 52.0 reduce-scatter.4
  213.1 100.9 all-gather.2
where the time goes:
time: 326 us
  waiting for transfers between devices  234 us (72%)
  blocking collectives  41.7 us (13%)
  starting transfers between devices  15.1 us (5%)
  between operations  13.9 us (4%)
  matrix products  8.36 us (3%)
  local copies, waits for them, and re-layouts  6.58 us (2%)
  other arithmetic  6.29 us (2%)
    reduce_scatter x2, waiting for transfers between devices, own_rows(): subtotal = lax.psum_scatter(subtotal, axis, scatter_dimension=0, tiled=True)  106 us
    all_gather x1, waiting for transfers between devices, local(): lax.all_gather(weights_half, FSDP, axis=0, tiled=True)  100 us
    all_gather x1, blocking collectives, side_by_side(): filled = lax.all_gather(both, axis, axis=dim, tiled=True)  41.7 us
    all_to_all x1, waiting for transfers between devices, copy_for_each(): return lax.all_to_all(copies, axis, split_axis=0, concat_axis=0, tiled=True)  13.7 us
    all_to_all x1, waiting for transfers between devices, sum_at_owner(): lax.all_to_all(tiles, axis, split_axis=0, concat_axis=0, tiled=True)  13.7 us
    all_to_all x1, starting transfers between devices, sum_at_owner(): lax.all_to_all(tiles, axis, split_axis=0, concat_axis=0, tiled=True)  7.73 us
    all_to_all x1, starting transfers between devices, copy_for_each(): return lax.all_to_all(copies, axis, split_axis=0, concat_axis=0, tiled=True)  7.26 us
  transfers between devices with their start and end apart: 5, of which 5 were waited for; matrix products, arithmetic and copies ran while one was open for 1% of the time, Pallas kernels for 0%

commit v1 on v0

v1 whole, which is shorter than its diff:
```python
import jax
import jax.numpy as jnp
from jax import lax
from jax.experimental import pallas as pl
from jax.experimental.pallas import tpu as pltpu
from jax.sharding import Mesh
from jax.sharding import PartitionSpec as P

MESH = pl.DeviceIdType.MESH
GRP = ("zl", "y", "core")
FSDP = ("x", "zh")

beta_one = 0.9
beta_two = 0.95
bias_one = 1.0 - 0.9**10
bias_two = 1.0 - 0.95**10
adam_eps = 1e-08
inner_rate = 0.01
weight_decay = 0.1
outer_rate = 0.7
outer_beta = 0.9
stat_eps = 1e-06

NC = 3
T = 128
bf16 = jnp.bfloat16
f32 = jnp.float32

XF, XD, XC, ZF, ZD, ZC = 0, 2, 4, 6, 8, 10
CE = 12
YS, LS, HS, AY, WY = 13, 16, 19, 22, 25
WX, WF, WC, AC = 28, 30, 32, 36
PER = 37
CX, CZ = NC * PER, NC * PER + 3
NSEM = NC * PER + 6


def kernel(
    tok, cot, wgt, omom, codes, frm, fcm, srm, scm,
    nw_o, nm_o, fs_o, ss_o, frm_o, fcm_o, srm_o, scm_o, keys_o,
    term, xr, cbuf, zf, zs, zr, zc, pf, pcs, pcr, ysf, ysb, yr, zlb, avgt, wbuf, acc,
    wf, rows, rmax, cmx, cmz, fnew, snew, ssem, rsem,
):
    x, zh = lax.axis_index("x"), lax.axis_index("zh")
    y, zl, c = lax.axis_index("y"), lax.axis_index("zl"), lax.axis_index("core")
    here = {"x": x, "zh": zh, "y": y, "zl": zl}

    def at(axis, offset):
        return lax.rem(here[axis] + (4 + offset), 4)

    def to(axis, offset):
        return {axis: at(axis, offset)}

    oc = 1 - c
    partner = {"core": oc}

    barrier = pltpu.get_barrier_semaphore()
    for axis in ("x", "zh", "y", "zl"):
        for o in (1, 2, 3):
            pl.semaphore_signal(barrier, inc=1, device_id=to(axis, o), device_id_type=MESH)
    pl.semaphore_signal(barrier, inc=1, device_id=partner, device_id_type=MESH)

    started = []

    def send(number, src, dst, device):
        copy = pltpu.make_async_remote_copy(
            src_ref=src, dst_ref=dst, send_sem=ssem.at[number], recv_sem=rsem.at[number],
            device_id=device, device_id_type=MESH,
        )
        copy.start()
        started.append(copy)

    def arrived(number, dst):
        pltpu.make_async_remote_copy(
            src_ref=dst, dst_ref=dst, send_sem=ssem.at[number], recv_sem=rsem.at[number],
            device_id=partner, device_id_type=MESH,
        ).wait_recv()

    def tile_columns(k, ab):
        return slice((2 * k + ab) * T, (2 * k + ab + 1) * T)

    def compute_term(k, slot, owner):
        @pl.loop(0, 4)
        def _(j):
            lhs = tok[0, :, pl.ds(pl.multiple_of(owner * 512 + j * T, T), T)]
            part = lax.dot_general(
                lhs, cot[0, :, 2 * k * T:(2 * k + 2) * T], (((0,), (0,)), ((), ())),
                preferred_element_type=f32,
            )
            at_rows = pl.ds(pl.multiple_of(j * T, T), T)
            term[k, slot, 0, at_rows, :] = part[:, :T].astype(bf16)
            term[k, slot, 1, at_rows, :] = part[:, T:].astype(bf16)

    def s0(k):
        compute_term(k, 0, at("x", 2))
        b = k * PER
        if k == 0:
            pl.semaphore_wait(barrier, 13)
        send(b + XF, term.at[k, 0, 0], xr.at[k, 0, 0], to("x", -1))
        send(b + XF + 1, term.at[k, 0, 1], xr.at[k, 0, 1], to("x", 1))

    def s1(k):
        b = k * PER
        compute_term(k, 1, at("x", 1))
        send(b + XD, term.at[k, 1, 0], xr.at[k, 1, 0], to("x", 1))
        compute_term(k, 2, at("x", -1))
        send(b + XD + 1, term.at[k, 2, 1], xr.at[k, 1, 1], to("x", -1))

    def s2(k):
        b = k * PER
        for ab, slot, way in ((0, 2, -1), (1, 1, 1)):
            arrived(b + XF + ab, xr.at[k, 0, ab])
            cbuf[k, ab] = (term[k, slot, ab].astype(f32) + xr[k, 0, ab].astype(f32)).astype(bf16)
            send(b + XC + ab, cbuf.at[k, ab], xr.at[k, 2, ab], to("x", way))

    def own_terms(k):
        compute_term(k, 3, x)

    def s3(k):
        b = k * PER
        for ab in (0, 1):
            arrived(b + XD + ab, xr.at[k, 1, ab])
        for ab in (0, 1):
            arrived(b + XC + ab, xr.at[k, 2, ab])

        def total(ab, block):
            at_rows = pl.ds(pl.multiple_of(block * T, T), T)
            value = (
                term[k, 3, ab, at_rows, :].astype(f32)
                + xr[k, 1, ab, at_rows, :].astype(f32)
                + xr[k, 2, ab, at_rows, :].astype(f32)
            )
            zf[k, ab, block] = value
            zs[k, ab, block] = value.astype(bf16)

        far, after, before = at("zh", 2), at("zh", 1), at("zh", -1)
        total(0, far)
        send(b + ZF, zs.at[k, 0, far], zr.at[k, 0, 0], to("zh", -1))
        total(1, far)
        send(b + ZF + 1, zs.at[k, 1, far], zr.at[k, 0, 1], to("zh", 1))
        total(0, after)
        send(b + ZD, zs.at[k, 0, after], zr.at[k, 1, 0], to("zh", 1))
        total(1, before)
        send(b + ZD + 1, zs.at[k, 1, before], zr.at[k, 1, 1], to("zh", -1))
        total(1, after)
        total(0, before)
        total(0, zh)
        total(1, zh)

    def s4(k):
        b = k * PER
        for ab, way in ((0, -1), (1, 1)):
            arrived(b + ZF + ab, zr.at[k, 0, ab])
            zc[k, ab] = (zf[k, ab, at("zh", way)] + zr[k, 0, ab].astype(f32)).astype(bf16)
            send(b + ZC + ab, zc.at[k, ab], zr.at[k, 2, ab], to("zh", way))

    def s5(k):
        b = k * PER
        for ab in (0, 1):
            arrived(b + ZD + ab, zr.at[k, 1, ab])
        for ab in (0, 1):
            arrived(b + ZC + ab, zr.at[k, 2, ab])
        for ab in (0, 1):
            cols = tile_columns(k, ab)
            gradient = zf[k, ab, zh] + zr[k, 1, ab].astype(f32) + zr[k, 2, ab].astype(f32)
            packed = codes[0, :, cols]
            first_code = (packed >> 4).astype(f32)
            second_code = (packed & 15).astype(f32)
            first_old = jnp.minimum(rows[0], fcm[:, cols]) * (first_code - 7.5) / 7.5
            level = (second_code + 1.0) / 16.0
            second_old = jnp.minimum(rows[1], scm[:, cols]) * (level * level)
            first_new = beta_one * first_old + (1.0 - beta_one) * gradient
            second_new = beta_two * second_old + (1.0 - beta_two) * gradient * gradient
            update = first_new / bias_one / (jnp.sqrt(second_new / bias_two) + adam_eps)
            pf[k, ab] = inner_rate * (update + weight_decay * wf[:, cols])
            fnew[:, cols] = first_new
            snew[:, cols] = second_new
            size = jnp.abs(first_new)
            cmx[x, 0:1, cols] = jnp.max(size, axis=0, keepdims=True)
            cmx[x, 1:2, cols] = jnp.max(second_new, axis=0, keepdims=True)
            if k == 0 and ab == 0:
                rmax[0] = size
                rmax[1] = second_new
            else:
                rmax[0] = jnp.maximum(rmax[0], size)
                rmax[1] = jnp.maximum(rmax[1], second_new)
        pcs[k] = pf[k, oc].astype(bf16)
        send(b + CE, pcs.at[k], pcr.at[k], partner)

    def s6(k):
        b = k * PER
        arrived(b + CE, pcr.at[k])
        both = pf[k, c] + pcr[k].astype(f32)
        ysf[k] = both
        ysb[k] = both.astype(bf16)
        for o in (1, 2, 3):
            theirs = pl.ds(pl.multiple_of(at("y", o) * 32, 32), 32)
            send(b + YS + o - 1, ysb.at[k, theirs, :], yr.at[k, o - 1], to("y", o))

    mine = pl.ds(pl.multiple_of(y * 32, 32), 32)

    def s7(k):
        b = k * PER
        for o in (1, 2, 3):
            arrived(b + YS + o - 1, yr.at[k, o - 1])
        zlb[k, zl] = (
            ysf[k, mine, :]
            + yr[k, 0].astype(f32) + yr[k, 1].astype(f32) + yr[k, 2].astype(f32)
        )
        for o in (1, 2, 3):
            send(b + LS + o - 1, zlb.at[k, zl], zlb.at[k, zl], to("zl", o))

    def s8(k):
        b = k * PER
        for o in (1, 2, 3):
            arrived(b + LS + o - 1, zlb.at[k, at("zl", -o)])
        averaged = ((zlb[k, 0] + zlb[k, 1]) + (zlb[k, 2] + zlb[k, 3])) / 32.0
        cols = pl.ds(pl.multiple_of((2 * k + c) * T, T), T)
        momentum = outer_beta * omom[mine, cols] + averaged
        weights = wf[mine, cols] - outer_rate * (averaged + outer_beta * momentum)
        wbuf[k, c, x, zh, mine, :] = weights.astype(bf16)
        for o in (2, 1, 3):
            piece = wbuf.at[k, c, x, zh, mine, :]
            send(b + HS + o - 1, piece, piece, to("zh", o))
        avgt[k, c, mine, :] = averaged
        for o in (1, 2, 3):
            piece = avgt.at[k, c, mine, :]
            send(b + AY + o - 1, piece, piece, to("y", o))

    def s9(k):
        b = k * PER
        for o in (1, 2, 3):
            arrived(b + HS + o - 1, wbuf.at[k, c, x, at("zh", -o), mine, :])
        for o in (2, 1, 3):
            piece = wbuf.at[k, c, x, :, mine, :]
            send(b + WY + o - 1, piece, piece, to("y", o))

    def s10(k):
        b = k * PER
        for o in (1, 2, 3):
            theirs = pl.ds(pl.multiple_of(at("y", -o) * 32, 32), 32)
            arrived(b + WY + o - 1, wbuf.at[k, c, x, :, theirs, :])
        block = wbuf.at[k, c, x]
        send(b + WX, block, block, to("x", 1))
        send(b + WX + 1, block, block, to("x", -1))
        send(b + WC, block, block, partner)

    def s11(k):
        b = k * PER
        before, after = at("x", -1), at("x", 1)
        arrived(b + WX, wbuf.at[k, c, before])
        part = wbuf.at[k, c, before, 0:2]
        send(b + WF, part, part, to("x", 1))
        arrived(b + WX + 1, wbuf.at[k, c, after])
        part = wbuf.at[k, c, after, 2:4]
        send(b + WF + 1, part, part, to("x", -1))
        for n, at_x in ((1, before), (2, after)):
            block = wbuf.at[k, c, at_x]
            send(b + WC + n, block, block, partner)

    def s12(k):
        b = k * PER
        far = at("x", 2)
        arrived(b + WF, wbuf.at[k, c, far, 0:2])
        arrived(b + WF + 1, wbuf.at[k, c, far, 2:4])
        block = wbuf.at[k, c, far]
        send(b + WC + 3, block, block, partner)

    def product(k, n, at_x):
        arrived(k * PER + WC + n, wbuf.at[k, oc, at_x])

        @pl.loop(0, 4)
        def _(j):
            at_rows = pl.ds(pl.multiple_of(j * T, T), T)
            lhs = tok[0, at_rows, pl.ds(pl.multiple_of(at_x * 512, 512), 512)]
            rhs = jnp.concatenate(
                [wbuf[k, 0, at_x].reshape(512, T), wbuf[k, 1, at_x].reshape(512, T)], axis=1
            )
            part = jnp.dot(lhs, rhs, preferred_element_type=f32)
            if n > 0:
                part = part + acc[k, at_rows, :]
            if n < 3:
                acc[k, at_rows, :] = part
            else:
                keys_o[0, at_rows, 2 * k * T:(2 * k + 2) * T] = part.astype(bf16)

    def near_products(k):
        product(k, 0, x)
        product(k, 1, at("x", -1))
        product(k, 2, at("x", 1))

    def s13(k):
        product(k, 3, at("x", 2))

    def t1(k):
        b = k * PER
        for o in (1, 2, 3):
            theirs = pl.ds(pl.multiple_of(at("y", -o) * 32, 32), 32)
            arrived(b + AY + o - 1, avgt.at[k, c, theirs, :])
        send(b + AC, avgt.at[k, c], avgt.at[k, c], partner)

    def t2(k):
        arrived(k * PER + AC, avgt.at[k, oc])
        for ab in (0, 1):
            cols = tile_columns(k, ab)
            averaged = avgt[k, ab]
            momentum = outer_beta * omom[:, cols] + averaged
            nm_o[:, cols] = momentum
            nw_o[:, cols] = wf[:, cols] - outer_rate * (averaged + outer_beta * momentum)

    def u0():
        for o in (1, 2, 3):
            send(CX + o - 1, cmx.at[x], cmx.at[x], to("x", o))

    def u1():
        for o in (1, 2, 3):
            arrived(CX + o - 1, cmx.at[at("x", -o)])
        cmz[zh] = jnp.maximum(jnp.maximum(cmx[0], cmx[1]), jnp.maximum(cmx[2], cmx[3]))
        for o in (1, 2, 3):
            send(CZ + o - 1, cmz.at[zh], cmz.at[zh], to("zh", o))

    def u2():
        for o in (1, 2, 3):
            arrived(CZ + o - 1, cmz.at[at("zh", -o)])
        cols_max = jnp.maximum(jnp.maximum(cmz[0], cmz[1]), jnp.maximum(cmz[2], cmz[3])) + stat_eps
        fcm_o[...] = cols_max[0:1]
        scm_o[...] = cols_max[1:2]
        for m, (new, rm_o, st_o) in enumerate(((fnew, frm_o, fs_o), (snew, srm_o, ss_o))):
            flipped = jnp.max(rmax[m].T, axis=0, keepdims=True) + stat_eps
            rm_o[...] = flipped
            rm = jnp.broadcast_to(flipped, (T, T)).T
            for t in range(2 * NC):
                cols = slice(t * T, (t + 1) * T)
                st_o[0, :, cols] = (
                    new[:, cols] / jnp.minimum(rm, cols_max[m:m + 1, cols])
                ).astype(bf16)

    s0(0)
    s1(0)
    s0(1)
    wf[...] = wgt[...].astype(f32)
    rows[0] = jnp.broadcast_to(frm[...], (T, T)).T
    rows[1] = jnp.broadcast_to(srm[...], (T, T)).T
    s2(0)
    s1(1)
    s0(2)
    s2(1)
    s1(2)
    own_terms(0)
    own_terms(1)
    own_terms(2)
    s3(0)
    s2(2)
    s4(0)
    s3(1)
    s5(0)
    s3(2)
    s6(0)
    s4(1)
    s7(0)
    s5(1)
    s4(2)
    s8(0)
    s6(1)
    s7(1)
    s5(2)
    u0()
    s6(2)
    s8(1)
    s9(0)
    s7(2)
    u1()
    s10(0)
    s8(2)
    s9(1)
    t1(0)
    s11(0)
    s10(1)
    t1(1)
    s12(0)
    near_products(0)
    s11(1)
    s9(2)
    s13(0)
    s12(1)
    near_products(1)
    s10(2)
    t1(2)
    s13(1)
    u2()
    t2(0)
    t2(1)
    t2(2)
    s11(2)
    product(2, 0, x)
    s12(2)
    product(2, 1, at("x", -1))
    product(2, 2, at("x", 1))
    s13(2)
    for copy in started:
        copy.wait_send()


def local(tok, cot, wgt, omom, codes, frm, fcm, srm, scm):
    def out(*shape, dtype=f32):
        return jax.ShapeDtypeStruct(shape, dtype)

    vmem = pl.BlockSpec(memory_space=pltpu.VMEM)
    return pl.pallas_call(
        kernel,
        out_shape=(
            out(128, 768), out(128, 768),
            out(1, 128, 768, dtype=bf16), out(1, 128, 768, dtype=bf16),
            out(1, 128), out(1, 768), out(1, 128), out(1, 768),
            out(1, 512, 768, dtype=bf16),
        ),
        in_specs=[vmem] * 9,
        out_specs=(vmem,) * 9,
        scratch_shapes=[
            pltpu.VMEM((NC, 4, 2, 512, T), bf16),
            pltpu.VMEM((NC, 3, 2, 512, T), bf16),
            pltpu.VMEM((NC, 2, 512, T), bf16),
            pltpu.VMEM((NC, 2, 4, T, T), f32),
            pltpu.VMEM((NC, 2, 4, T, T), bf16),
            pltpu.VMEM((NC, 3, 2, T, T), bf16),
            pltpu.VMEM((NC, 2, T, T), bf16),
            pltpu.VMEM((NC, 2, T, T), f32),
            pltpu.VMEM((NC, T, T), bf16),
            pltpu.VMEM((NC, T, T), bf16),
            pltpu.VMEM((NC, T, T), f32),
            pltpu.VMEM((NC, T, T), bf16),
            pltpu.VMEM((NC, 3, 32, T), bf16),
            pltpu.VMEM((NC, 4, 32, T), f32),
            pltpu.VMEM((NC, 2, T, T), f32),
            pltpu.VMEM((NC, 2, 4, 4, T, T), bf16),
            pltpu.VMEM((NC, 512, 2 * T), f32),
            pltpu.VMEM((T, 768), f32),
            pltpu.VMEM((2, T, T), f32),
            pltpu.VMEM((2, T, T), f32),
            pltpu.VMEM((4, 2, 768), f32),
            pltpu.VMEM((4, 2, 768), f32),
            pltpu.VMEM((T, 768), f32),
            pltpu.VMEM((T, 768), f32),
            pltpu.SemaphoreType.DMA((NSEM,)),
            pltpu.SemaphoreType.DMA((NSEM,)),
        ],
        compiler_params=pltpu.CompilerParams(
            collective_id=0, has_side_effects=True, vmem_limit_bytes=48 * 1024 * 1024
        ),
        name="round",
    )(tok, cot, wgt, omom, codes, frm, fcm, srm, scm)


def solution(mesh):
    finer = Mesh(mesh.devices.reshape(4, 4, 2, 4, 4), (*GRP, *FSDP))
    in_specs = (
        P(GRP, FSDP, None), P(GRP, FSDP, None), P(FSDP, None), P(FSDP, None),
        P(GRP, FSDP, None), P(GRP, FSDP), P(GRP, None), P(GRP, FSDP), P(GRP, None),
    )
    out_specs = (
        P(FSDP, None), P(FSDP, None), P(GRP, FSDP, None), P(GRP, FSDP, None),
        P(GRP, FSDP), P(GRP, None), P(GRP, FSDP), P(GRP, None), P(GRP, FSDP, None),
    )
    return jax.shard_map(local, mesh=finer, in_specs=in_specs, out_specs=out_specs, check_vma=False)
```

time: 326 us -> 117 us (0.36)
  waiting for transfers between devices: 234 us -> 0 us
  Pallas kernels: 0 us -> 102 us
  blocking collectives: 41.7 us -> 0 us
  starting transfers between devices: 15.1 us -> 0 us
  between operations: 13.9 us -> 0.67 us
  matrix products: 8.36 us -> 0 us
  local copies, waits for them, and re-layouts: 6.58 us -> 14.2 us
  other arithmetic: 6.29 us -> 0 us
    reduce_scatter x2 -> x0, waiting for transfers between devices: 106 us -> none  [own_rows(): subtotal = lax.psum_scatter(subtotal, axis, scatter_dimension=0, tiled=True)]
    pallas_call x0 -> x1, Pallas kernels: none -> 102 us  [local(): pl.pallas_call(kernel, out_shape=(out(128, 768), out(128, 768), out(1, 12...]
    all_gather x1 -> x0, waiting for transfers between devices: 100 us -> none  [local(): lax.all_gather(weights_half, FSDP, axis=0, tiled=True)]
    all_gather x1 -> x0, blocking collectives: 41.7 us -> none  [side_by_side(): filled = lax.all_gather(both, axis, axis=dim, tiled=True)]
    all_to_all x2 -> x0, waiting for transfers between devices: 27.4 us -> none  [the longest x1 13.7 us: copy_for_each(): return lax.all_to_all(copies, axis, split_axis=0, concat_axis=0, tiled=True)]
    all_to_all x2 -> x0, starting transfers between devices: 15 us -> none  [the longest x1 7.73 us: sum_at_owner(): lax.all_to_all(tiles, axis, split_axis=0, concat_axis=0, tiled=True)]
    unnamed x16 -> x27, local copies, waits for them, and re-layouts: 3.87 us -> 14.2 us
    dot_general x2 -> x0, matrix products: 8.36 us -> none  [the longest x1 4.64 us: local(): lax.dot_general(columns, cotangent, (((0,), (0,)), ((), ())), preferred_e...]
  transfers between devices with their start and end apart: 5 -> 0, of which waited for: 5 -> 0; matrix products, arithmetic and copies ran while one was open for 1% -> 0% of each run, Pallas kernels for 0% -> 0%
where the time goes in v1:
time: 117 us
  Pallas kernels  102 us (87%)
  local copies, waits for them, and re-layouts  14.2 us (12%)
    pallas_call x1, Pallas kernels, local(): pl.pallas_call(kernel, out_shape=(out(128, 768), out(128, 768), out(1, 12...  102 us
    unnamed x27, local copies, waits for them, and re-layouts  14.2 us

profile of v1, /device:TPU:1, one launch (start us, length us, event | category | flops | bytes accessed | tf_op | source)
XLA Modules:
  0.0 117.0 jit_solution(17622526367205389192)
XLA Ops:
  0.6 0.0 copy-start
  0.7 1.6 %copy-done = bf16[1,512,2048]{2,1,0:T(8,128)(2,1)S(1)} copy-done((bf16[1,512,2048]{2,1,0:T(8,128)(2,1)S(1)}, bf16[1,512,2048]{2,1,0:T(8,128)(2,1)}, u32[]{:S(2)}) %copy-start) | copy-done | bytes 2097176
  2.2 0.0 copy-start.1
  2.2 1.1 copy-done.1
  3.4 0.0 copy-start.2
  3.4 1.0 copy-done.2
  4.4 0.0 copy-start.3
  4.4 1.0 copy-done.3
  5.4 0.0 copy-start.4
  5.4 0.9 copy-done.4
  6.3 0.7 copy-done.5
  7.0 0.7 copy-done.6
  7.7 0.7 copy-done.7
  8.3 0.7 copy-done.8
  9.0 102.1 %round.1 = (f32[128,768]{1,0:T(8,128)S(1)}, f32[128,768]{1,0:T(8,128)S(1)}, bf16[1,128,768]{2,1,0:T(8,128)(2,1)S(1)}, bf16[1,128,768]{2,1,0:T(8,128)(2,1)S(1)}, ...) custom-call(bf16[1,512,2048]{2,1,0:T(8,128)(2,1)S(1)} %copy-done, ...), custom_call_target="tpu_custom_call" | custom-call | tf_op jit(solution)/shard_map/round/pallas_call | solution.py:409
  111.1 0.7 copy.27
  111.8 0.7 copy.28
  112.6 0.7 copy.29
  113.2 0.7 copy.30
  113.9 0.5 copy.31
  114.4 0.6 copy.32
  115.0 0.5 copy.33
  115.5 0.6 copy.34
  116.1 0.9 copy.35
  (4 shorter events, 0.0 us)
Async XLA Ops:
  0.6 1.6 %copy-start = (bf16[1,512,2048]{2,1,0:T(8,128)(2,1)S(1)}, bf16[1,512,2048]{2,1,0:T(8,128)(2,1)}, u32[]{:S(2)}) copy-start(bf16[1,512,2048]{2,1,0:T(8,128)(2,1)} %tok.1) | copy-start | bytes 6291460
  2.2 1.1 copy-start.1
  3.4 1.0 copy-start.2
  4.4 1.0 copy-start.3
  5.4 0.9 copy-start.4
  6.3 0.7 copy-start.5
  7.0 0.7 copy-start.6
  7.7 0.7 copy-start.7
  8.3 0.7 copy-start.8

commit v2 on v1

v2 whole, which is shorter than its diff:
```python
import jax
import jax.numpy as jnp
from jax import lax
from jax.experimental import pallas as pl
from jax.experimental.pallas import tpu as pltpu
from jax.sharding import Mesh
from jax.sharding import PartitionSpec as P

MESH = pl.DeviceIdType.MESH
GRP = ("zl", "y", "core")
FSDP = ("x", "zh")

beta_one = 0.9
beta_two = 0.95
bias_one = 1.0 - 0.9**10
bias_two = 1.0 - 0.95**10
adam_eps = 1e-08
inner_rate = 0.01
weight_decay = 0.1
outer_rate = 0.7
outer_beta = 0.9
stat_eps = 1e-06

NC = 6
T = 128
H = 64
Q = 16
bf16 = jnp.bfloat16
f32 = jnp.float32

XF, XD, XC, ZF, ZD, ZC = 0, 2, 4, 6, 8, 10
CE = 12
YS, LS, HS, AY, WY = 13, 16, 19, 22, 25
WX, WF, WC, AC = 28, 30, 32, 36
PER = 37
CX, CZ = NC * PER, NC * PER + 3
NSEM = NC * PER + 6

SCHEDULE = (
    "ta:0", "s0:0", "tc:0", "tb:2", "tc:2", "s0:1", "ta:2", "s0:2", "tb:0", "s1:0", "s2:0",
    "s2:1", "tb:4", "tc:4", "s1:1", "s2:2", "td:0", "s1:2", "ta:4", "s0:3", "s3:0", "prepare",
    "s3:1", "s0:4", "td:2", "s3:2", "s0:5", "s2:3", "s1:3", "s2:4", "s4:0", "s4:1", "s1:4",
    "s1:5", "s4:2", "s3:3", "s2:5", "td:4", "s3:4", "s3:5", "s5:0", "s5:1", "s6:1", "s6:0",
    "s5:2", "peaks:0", "peaks:1", "s4:3", "s6:2", "s4:4", "s7:1", "s7:0", "s4:5", "peaks:2",
    "s7:2", "s5:3", "s5:4", "peaks:3", "s6:3", "s8:0", "peaks:4", "s6:4", "s8:1", "s5:5",
    "peaks:5", "s8:2", "s6:5", "s7:3", "s7:4", "s7:5", "u0", "s8:3", "s9:0", "s8:4", "s9:1",
    "s8:5", "s9:2", "s10:0", "t1:2", "s10:1", "s10:2", "t1:3", "t1:4", "t1:1", "s9:3", "s9:4",
    "s11:0", "s11:1", "u1", "s9:5", "s11:2", "t2:4", "s10:3", "s12:0", "t2:1", "s10:4", "s10:5",
    "pa:4", "s12:1", "t1:0", "s12:2", "s11:3", "t2:3", "t2:2", "t1:5", "s11:4", "both:0",
    "s11:5", "pa:5", "u2", "s12:3", "pb:4", "t2:0", "t2:5", "s12:4", "pb:5", "s12:5", "both:2",
    "pc:4", "pc:5",
)


def kernel(
    tok_h, cot_h, wgt_h, omom_h, codes_h, frm_h, fcm_h, srm_h, scm_h,
    nw_h, nm_h, fs_h, ss_h, frmo_h, fcmo_h, srmo_h, scmo_h, keys_h,
    tok, cot, wgt, omom, codes, frm, fcm, srm, scm, insem,
    nw_o, nm_o, fs_o, ss_o, frm_o, fcm_o, srm_o, scm_o, keys_o, outsem,
    term, xr, cbuf, zf, zs, zr, zc, pf, pcs, pcr, ysf, ysb, yr, zlb, avgt, wbuf, acc,
    wf, rows, rmax, cmx, cmz, fnew, snew, ssem, rsem,
):
    x, zh = lax.axis_index("x"), lax.axis_index("zh")
    y, zl, c = lax.axis_index("y"), lax.axis_index("zl"), lax.axis_index("core")
    here = {"x": x, "zh": zh, "y": y, "zl": zl}

    def at(axis, offset):
        return lax.rem(here[axis] + (4 + offset), 4)

    def to(axis, offset):
        return {axis: at(axis, offset)}

    oc = 1 - c
    partner = {"core": oc}

    barrier = pltpu.get_barrier_semaphore()
    for axis in ("zh", "zl", "y", "x"):
        for o in (2, 1, 3):
            pl.semaphore_signal(barrier, inc=1, device_id=to(axis, o), device_id_type=MESH)
    pl.semaphore_signal(barrier, inc=1, device_id=partner, device_id_type=MESH)

    def token_columns(owner):
        return pl.ds(pl.multiple_of(owner * 512, 512), 512)

    def token_copy(n, owner):
        cols = token_columns(owner)
        return pltpu.make_async_copy(tok_h.at[0, :, cols], tok.at[0, :, cols], insem.at[n])

    owners = (at("x", 2), at("x", 1), at("x", -1), x)
    cot_copy = pltpu.make_async_copy(cot_h, cot, insem.at[4])
    small_copies = [
        pltpu.make_async_copy(src, dst, insem.at[5 + n])
        for n, (src, dst) in enumerate((
            (codes_h, codes), (wgt_h, wgt), (omom_h, omom),
            (frm_h, frm), (fcm_h, fcm), (srm_h, srm), (scm_h, scm),
        ))
    ]
    cot_copy.start()
    for n in range(4):
        token_copy(n, owners[n]).start()
    for copy in small_copies:
        copy.start()

    started, leaving = [], []

    def send(number, src, dst, device):
        copy = pltpu.make_async_remote_copy(
            src_ref=src, dst_ref=dst, send_sem=ssem.at[number], recv_sem=rsem.at[number],
            device_id=device, device_id_type=MESH,
        )
        copy.start()
        started.append(copy)

    def arrived(number, dst):
        pltpu.make_async_remote_copy(
            src_ref=dst, dst_ref=dst, send_sem=ssem.at[number], recv_sem=rsem.at[number],
            device_id=partner, device_id_type=MESH,
        ).wait_recv()

    def leave(src, dst):
        copy = pltpu.make_async_copy(src, dst, outsem.at[len(leaving)])
        copy.start()
        leaving.append(copy)

    def columns(k, n=1):
        return slice(k * T, (k + n) * T)

    def rows_of(start, size):
        return pl.ds(pl.multiple_of(start, size), size)

    def terms(slot, first, count):
        owner = owners[slot]
        part = lax.dot_general(
            tok[0, :, token_columns(owner)], cot[0, :, columns(first, count)],
            (((0,), (0,)), ((), ())), preferred_element_type=f32,
        ).astype(bf16)
        for n in range(count):
            for block in range(4):
                for ab in (0, 1):
                    r = block * T + ab * H
                    term[first + n, slot, ab, block] = part[r:r + H, columns(n)]

    loaded = set()

    def first_terms(slot, k):
        if not loaded:
            cot_copy.wait()
        if slot not in loaded:
            token_copy(slot, owners[slot]).wait()
            loaded.add(slot)
        terms(slot, k, 2)

    def ta(k):
        first_terms(0, k)

    def tb(k):
        first_terms(1, k)

    def tc(k):
        first_terms(2, k)

    def td(k):
        first_terms(3, k)

    def prepare():
        for copy in small_copies:
            copy.wait()
        wf[...] = wgt[...].astype(f32)
        rows[0] = jnp.broadcast_to(frm[...], (T, T)).T
        rows[1] = jnp.broadcast_to(srm[...], (T, T)).T

    def s0(k):
        b = k * PER
        if k == 0:
            pl.semaphore_wait(barrier, 13)
        send(b + XF, term.at[k, 0, 0], xr.at[k, 0, 0], to("x", -1))
        send(b + XF + 1, term.at[k, 0, 1], xr.at[k, 0, 1], to("x", 1))

    def s1(k):
        b = k * PER
        send(b + XD, term.at[k, 1, 0], xr.at[k, 1, 0], to("x", 1))
        send(b + XD + 1, term.at[k, 2, 1], xr.at[k, 1, 1], to("x", -1))

    def s2(k):
        b = k * PER
        for ab, slot, way in ((0, 2, -1), (1, 1, 1)):
            arrived(b + XF + ab, xr.at[k, 0, ab])
            cbuf[k, ab] = (term[k, slot, ab].astype(f32) + xr[k, 0, ab].astype(f32)).astype(bf16)
            send(b + XC + ab, cbuf.at[k, ab], xr.at[k, 2, ab], to("x", way))

    def s3(k):
        b = k * PER
        for ab in (0, 1):
            arrived(b + XD + ab, xr.at[k, 1, ab])
        for ab in (0, 1):
            arrived(b + XC + ab, xr.at[k, 2, ab])

        def total(ab, block):
            value = (
                term[k, 3, ab, block].astype(f32)
                + xr[k, 1, ab, block].astype(f32)
                + xr[k, 2, ab, block].astype(f32)
            )
            zf[k, ab, block] = value
            zs[k, ab, block] = value.astype(bf16)

        far, after, before = at("zh", 2), at("zh", 1), at("zh", -1)
        total(0, far)
        send(b + ZF, zs.at[k, 0, far], zr.at[k, 0, 0], to("zh", -1))
        total(1, far)
        send(b + ZF + 1, zs.at[k, 1, far], zr.at[k, 0, 1], to("zh", 1))
        total(0, after)
        send(b + ZD, zs.at[k, 0, after], zr.at[k, 1, 0], to("zh", 1))
        total(1, before)
        send(b + ZD + 1, zs.at[k, 1, before], zr.at[k, 1, 1], to("zh", -1))
        total(1, after)
        total(0, before)
        total(0, zh)
        total(1, zh)

    def s4(k):
        b = k * PER
        for ab, way in ((0, -1), (1, 1)):
            arrived(b + ZF + ab, zr.at[k, 0, ab])
            zc[k, ab] = (zf[k, ab, at("zh", way)] + zr[k, 0, ab].astype(f32)).astype(bf16)
            send(b + ZC + ab, zc.at[k, ab], zr.at[k, 2, ab], to("zh", way))

    def s5(k):
        b = k * PER
        for ab in (0, 1):
            arrived(b + ZD + ab, zr.at[k, 1, ab])
        for ab in (0, 1):
            arrived(b + ZC + ab, zr.at[k, 2, ab])
        cols = columns(k)
        for ab in (0, 1):
            half = slice(ab * H, (ab + 1) * H)
            gradient = zf[k, ab, zh] + zr[k, 1, ab].astype(f32) + zr[k, 2, ab].astype(f32)
            packed = codes[0, half, cols]
            first_code = (packed >> 4).astype(f32)
            second_code = (packed & 15).astype(f32)
            first_old = jnp.minimum(rows[0, half], fcm[:, cols]) * (first_code - 7.5) / 7.5
            level = (second_code + 1.0) / 16.0
            second_old = jnp.minimum(rows[1, half], scm[:, cols]) * (level * level)
            first_new = beta_one * first_old + (1.0 - beta_one) * gradient
            second_new = beta_two * second_old + (1.0 - beta_two) * gradient * gradient
            update = first_new / bias_one / (jnp.sqrt(second_new / bias_two) + adam_eps)
            pf[k, ab] = inner_rate * (update + weight_decay * wf[half, cols])
            fnew[half, cols] = first_new
            snew[half, cols] = second_new
        pcs[k] = pf[k, oc].astype(bf16)
        send(b + CE, pcs.at[k], pcr.at[k], partner)

    def peaks(k):
        cols = columns(k)
        for m, value in enumerate((jnp.abs(fnew[:, cols]), snew[:, cols])):
            cmx[x, m:m + 1, cols] = jnp.max(value, axis=0, keepdims=True)
            rmax[m] = value if k == 0 else jnp.maximum(rmax[m], value)

    def s6(k):
        b = k * PER
        arrived(b + CE, pcr.at[k])
        both = pf[k, c] + pcr[k].astype(f32)
        ysf[k] = both
        ysb[k] = both.astype(bf16)
        for o in (2, 1, 3):
            theirs = rows_of(at("y", o) * Q, Q)
            send(b + YS + o - 1, ysb.at[k, theirs, :], yr.at[k, o - 1], to("y", o))

    mine = rows_of(y * Q, Q)
    mine_of_block = rows_of(c * H + y * Q, Q)
    my_half = rows_of(c * H, H)
    other_half = rows_of(oc * H, H)

    def s7(k):
        b = k * PER
        for o in (1, 2, 3):
            arrived(b + YS + o - 1, yr.at[k, o - 1])
        zlb[k, zl] = (
            ysf[k, mine, :]
            + yr[k, 0].astype(f32) + yr[k, 1].astype(f32) + yr[k, 2].astype(f32)
        ).astype(bf16)
        for o in (1, 2, 3):
            send(b + LS + o - 1, zlb.at[k, zl], zlb.at[k, zl], to("zl", o))

    def s8(k):
        b = k * PER
        for o in (1, 2, 3):
            arrived(b + LS + o - 1, zlb.at[k, at("zl", -o)])
        parts = [zlb[k, n].astype(f32) for n in range(4)]
        averaged = ((parts[0] + parts[1]) + (parts[2] + parts[3])) / 32.0
        cols = columns(k)
        momentum = outer_beta * omom[mine_of_block, cols] + averaged
        weights = wf[mine_of_block, cols] - outer_rate * (averaged + outer_beta * momentum)
        wbuf[k, x, zh, mine_of_block, :] = weights.astype(bf16)
        for o in (2, 1, 3):
            piece = wbuf.at[k, x, zh, mine_of_block, :]
            send(b + HS + o - 1, piece, piece, to("zh", o))
        avgt[k, mine_of_block, :] = averaged
        for o in (1, 2, 3):
            piece = avgt.at[k, mine_of_block, :]
            send(b + AY + o - 1, piece, piece, to("y", o))

    def s9(k):
        b = k * PER
        for o in (1, 2, 3):
            arrived(b + HS + o - 1, wbuf.at[k, x, at("zh", -o), mine_of_block, :])
        for o in (2, 1, 3):
            piece = wbuf.at[k, x, :, mine_of_block, :]
            send(b + WY + o - 1, piece, piece, to("y", o))

    def half_block(k, at_x, zhs=slice(None)):
        return wbuf.at[k, at_x, zhs, my_half, :]

    def s10(k):
        b = k * PER
        for o in (1, 2, 3):
            theirs = rows_of(c * H + at("y", -o) * Q, Q)
            arrived(b + WY + o - 1, wbuf.at[k, x, :, theirs, :])
        block = half_block(k, x)
        send(b + WX, block, block, to("x", 1))
        send(b + WX + 1, block, block, to("x", -1))
        send(b + WC, block, block, partner)

    def s11(k):
        b = k * PER
        before, after = at("x", -1), at("x", 1)
        arrived(b + WX, half_block(k, before))
        part = half_block(k, before, slice(0, 2))
        send(b + WF, part, part, to("x", 1))
        arrived(b + WX + 1, half_block(k, after))
        part = half_block(k, after, slice(2, 4))
        send(b + WF + 1, part, part, to("x", -1))
        for n, at_x in ((1, before), (2, after)):
            block = half_block(k, at_x)
            send(b + WC + n, block, block, partner)

    def s12(k):
        b = k * PER
        far = at("x", 2)
        arrived(b + WF, half_block(k, far, slice(0, 2)))
        arrived(b + WF + 1, half_block(k, far, slice(2, 4)))
        block = half_block(k, far)
        send(b + WC + 3, block, block, partner)

    def from_partner(k, n, at_x):
        arrived(k * PER + WC + n, wbuf.at[k, at_x, :, other_half, :])

    def block_of(k, at_x):
        return wbuf[k, at_x].reshape(512, T)

    places = (x, at("x", -1), at("x", 1), at("x", 2))

    def product(k, count):
        for n in range(count):
            for i in range(4):
                from_partner(k + n, i, places[i])
        total = None
        for at_x in range(4):
            rhs = jnp.concatenate([block_of(k + n, at_x) for n in range(count)], axis=1)
            part = jnp.dot(tok[0, :, at_x * 512:(at_x + 1) * 512], rhs, preferred_element_type=f32)
            total = part if total is None else total + part
        keys_o[0, :, columns(k, count)] = total.astype(bf16)
        leave(keys_o.at[0, :, columns(k, count)], keys_h.at[0, :, columns(k, count)])

    def both(k):
        product(k, 2)

    def partial(k, i):
        from_partner(k, i, places[i])
        part = jnp.dot(
            tok[0, :, token_columns(places[i])], block_of(k, places[i]),
            preferred_element_type=f32,
        )
        if i > 0:
            part = part + acc[k - NC + 2]
        if i < 3:
            acc[k - NC + 2] = part
        else:
            keys_o[0, :, columns(k)] = part.astype(bf16)
            leave(keys_o.at[0, :, columns(k)], keys_h.at[0, :, columns(k)])

    def pa(k):
        partial(k, 0)

    def pb(k):
        partial(k, 1)
        partial(k, 2)

    def pc(k):
        partial(k, 3)

    def t1(k):
        b = k * PER
        for o in (1, 2, 3):
            theirs = rows_of(c * H + at("y", -o) * Q, Q)
            arrived(b + AY + o - 1, avgt.at[k, theirs, :])
        piece = avgt.at[k, my_half, :]
        send(b + AC, piece, piece, partner)

    def t2(k):
        arrived(k * PER + AC, avgt.at[k, other_half, :])
        cols = columns(k)
        averaged = avgt[k]
        momentum = outer_beta * omom[:, cols] + averaged
        nm_o[:, cols] = momentum
        nw_o[:, cols] = wf[:, cols] - outer_rate * (averaged + outer_beta * momentum)
        if k == NC - 1:
            leave(nm_o, nm_h)
            leave(nw_o, nw_h)

    def u0():
        for o in (1, 2, 3):
            send(CX + o - 1, cmx.at[x], cmx.at[x], to("x", o))

    def u1():
        for o in (1, 2, 3):
            arrived(CX + o - 1, cmx.at[at("x", -o)])
        cmz[zh] = jnp.maximum(jnp.maximum(cmx[0], cmx[1]), jnp.maximum(cmx[2], cmx[3]))
        for o in (1, 2, 3):
            send(CZ + o - 1, cmz.at[zh], cmz.at[zh], to("zh", o))

    def u2():
        for o in (1, 2, 3):
            arrived(CZ + o - 1, cmz.at[at("zh", -o)])
        cols_max = jnp.maximum(jnp.maximum(cmz[0], cmz[1]), jnp.maximum(cmz[2], cmz[3])) + stat_eps
        fcm_o[...] = cols_max[0:1]
        scm_o[...] = cols_max[1:2]
        leave(fcm_o, fcmo_h)
        leave(scm_o, scmo_h)
        for m, (new, rm_o, rm_h, st_o, st_h) in enumerate(
            ((fnew, frm_o, frmo_h, fs_o, fs_h), (snew, srm_o, srmo_h, ss_o, ss_h))
        ):
            flipped = jnp.max(rmax[m].T, axis=0, keepdims=True) + stat_eps
            rm_o[...] = flipped
            leave(rm_o, rm_h)
            rm = jnp.broadcast_to(flipped, (T, T)).T
            for k in range(NC):
                cols = columns(k)
                st_o[0, :, cols] = (
                    new[:, cols] / jnp.minimum(rm, cols_max[m:m + 1, cols])
                ).astype(bf16)
            leave(st_o, st_h)

    stages = {
        f.__name__: f
        for f in (
            ta, tb, tc, td, prepare, s0, s1, s2, s3, s4, s5, peaks, s6, s7, s8, s9, s10, s11, s12,
            both, pa, pb, pc, t1, t2, u0, u1, u2,
        )
    }
    for entry in SCHEDULE:
        name, *chunk = entry.split(":")
        with jax.named_scope("_".join([name, *chunk])):
            stages[name](*map(int, chunk))
    for copy in started:
        copy.wait_send()
    for copy in leaving:
        copy.wait()


def deliver(*refs):
    sources, targets, held, arrive, depart = refs[:9], refs[9:18], refs[18:27], refs[27], refs[28]
    inward = [pltpu.make_async_copy(src, mid, arrive.at[n]) for n, (src, mid) in enumerate(zip(sources, held))]
    outward = [pltpu.make_async_copy(mid, dst, depart.at[n]) for n, (mid, dst) in enumerate(zip(held, targets))]
    for copy in inward:
        copy.start()
    for into, out in zip(inward, outward):
        into.wait()
        out.start()
    for copy in outward:
        copy.wait()


def local(tok, cot, wgt, omom, codes, frm, fcm, srm, scm):
    def out(*shape, dtype=f32):
        return jax.ShapeDtypeStruct(shape, dtype)

    hbm = pl.BlockSpec(memory_space=pl.ANY)
    outs = (
        out(128, 768), out(128, 768),
        out(1, 128, 768, dtype=bf16), out(1, 128, 768, dtype=bf16),
        out(1, 128), out(1, 768), out(1, 128), out(1, 768),
        out(1, 512, 768, dtype=bf16),
    )
    arguments = (tok, cot, wgt, omom, codes, frm, fcm, srm, scm)
    results = pl.pallas_call(
        kernel,
        out_shape=outs,
        in_specs=[hbm] * 9,
        out_specs=(hbm,) * 9,
        scratch_shapes=[
            *(pltpu.VMEM(a.shape, a.dtype) for a in arguments),
            pltpu.SemaphoreType.DMA((12,)),
            *(pltpu.VMEM(a.shape, a.dtype) for a in outs),
            pltpu.SemaphoreType.DMA((16,)),
            pltpu.VMEM((NC, 4, 2, 4, H, T), bf16),
            pltpu.VMEM((NC, 3, 2, 4, H, T), bf16),
            pltpu.VMEM((NC, 2, 4, H, T), bf16),
            pltpu.VMEM((NC, 2, 4, H, T), f32),
            pltpu.VMEM((NC, 2, 4, H, T), bf16),
            pltpu.VMEM((NC, 3, 2, H, T), bf16),
            pltpu.VMEM((NC, 2, H, T), bf16),
            pltpu.VMEM((NC, 2, H, T), f32),
            pltpu.VMEM((NC, H, T), bf16),
            pltpu.VMEM((NC, H, T), bf16),
            pltpu.VMEM((NC, H, T), f32),
            pltpu.VMEM((NC, H, T), bf16),
            pltpu.VMEM((NC, 3, Q, T), bf16),
            pltpu.VMEM((NC, 4, Q, T), bf16),
            pltpu.VMEM((NC, T, T), f32),
            pltpu.VMEM((NC, 4, 4, T, T), bf16),
            pltpu.VMEM((2, 512, T), f32),
            pltpu.VMEM((T, 768), f32),
            pltpu.VMEM((2, T, T), f32),
            pltpu.VMEM((2, T, T), f32),
            pltpu.VMEM((4, 2, 768), f32),
            pltpu.VMEM((4, 2, 768), f32),
            pltpu.VMEM((T, 768), f32),
            pltpu.VMEM((T, 768), f32),
            pltpu.SemaphoreType.DMA((NSEM,)),
            pltpu.SemaphoreType.DMA((NSEM,)),
        ],
        compiler_params=pltpu.CompilerParams(
            collective_id=0, has_side_effects=True, vmem_limit_bytes=67043328
        ),
        name="round",
    )(*arguments)
    return pl.pallas_call(
        deliver,
        out_shape=outs,
        in_specs=[hbm] * 9,
        out_specs=(hbm,) * 9,
        scratch_shapes=[
            *(pltpu.VMEM(a.shape, a.dtype) for a in outs),
            pltpu.SemaphoreType.DMA((9,)),
            pltpu.SemaphoreType.DMA((9,)),
        ],
        compiler_params=pltpu.CompilerParams(vmem_limit_bytes=67043328),
        name="deliver",
    )(*results)


def solution(mesh):
    finer = Mesh(mesh.devices.reshape(4, 4, 2, 4, 4), (*GRP, *FSDP))
    in_specs = (
        P(GRP, FSDP, None), P(GRP, FSDP, None), P(FSDP, None), P(FSDP, None),
        P(GRP, FSDP, None), P(GRP, FSDP), P(GRP, None), P(GRP, FSDP), P(GRP, None),
    )
    out_specs = (
        P(FSDP, None), P(FSDP, None), P(GRP, FSDP, None), P(GRP, FSDP, None),
        P(GRP, FSDP), P(GRP, None), P(GRP, FSDP), P(GRP, None), P(GRP, FSDP, None),
    )
    return jax.shard_map(local, mesh=finer, in_specs=in_specs, out_specs=out_specs, check_vma=False)
```

time: 117 us -> 93.7 us (0.80)
  local copies, waits for them, and re-layouts: 14.2 us -> 0 us
  Pallas kernels: 102 us -> 92.9 us
    unnamed x27 -> x0, local copies, waits for them, and re-layouts: 14.2 us -> none
    pallas_call x1 -> x2, Pallas kernels: 102 us -> 92.9 us  [the longest x1 90.4 us: local(): pl.pallas_call(kernel, out_shape=outs, in_specs=[hbm] * 9, out_specs=(hbm...]
where the time goes in v2:
time: 93.7 us; the launch traced here: 93.6 us
  Pallas kernels  92.9 us (99%)
    pallas_call x1, Pallas kernels, local(): pl.pallas_call(kernel, out_shape=outs, in_specs=[hbm] * 9, out_specs=(hbm...  90.4 us
    pallas_call x1, Pallas kernels, local(): pl.pallas_call(deliver, out_shape=outs, in_specs=[hbm] * 9, out_specs=(hb...  2.56 us

profile of v2, /device:TPU:1, one launch (start us, length us, event | category | flops | bytes accessed | tf_op | source)
XLA Modules:
  0.0 93.6 jit_solution(14045645987167195741)
XLA Ops:
  0.6 90.4 %round.1 = (f32[128,768]{1,0:T(8,128)}, f32[128,768]{1,0:T(8,128)}, bf16[1,128,768]{2,1,0:T(8,128)(2,1)}, bf16[1,128,768]{2,1,0:T(8,128)(2,1)}, f32[1,128]{1,0:T...) custom-call(bf16[1,512,2048]{2,1,0:T(8,128)(2,1)} %tok_h.1, ...), custom_call_target="tpu_custom_call" | custom-call | tf_op jit(solution)/shard_map/round/pallas_call | solution.py:486
  91.0 2.6 %deliver.1 = (f32[128,768]{1,0:T(8,128)}, f32[128,768]{1,0:T(8,128)}, bf16[1,128,768]{2,1,0:T(8,128)(2,1)}, bf16[1,128,768]{2,1,0:T(8,128)(2,1)}, f32[1,128]{1,0...) custom-call(f32[128,768]{1,0:T(8,128)} %get-tuple-element.18.refs_0_, ...), custom_call_target="tpu_custom_call" | custom-call | tf_op jit(solution)/shard_map/deliver/pallas_call | solution.py:528

commit v3 on v2

--- a/solution.py
+++ b/solution.py
@@ -28,27 +28,28 @@
 bf16 = jnp.bfloat16
 f32 = jnp.float32
 
-XF, XD, XC, ZF, ZD, ZC = 0, 2, 4, 6, 8, 10
-CE = 12
-YS, LS, HS, AY, WY = 13, 16, 19, 22, 25
-WX, WF, WC, AC = 28, 30, 32, 36
-PER = 37
+XF, XD, XC, ZF, ZD, ZC = 0, 4, 8, 12, 14, 16
+YS, LS, HS, AY, WY = 18, 25, 28, 31, 34
+WX, WF, WC, AC = 37, 39, 41, 45
+PER = 46
 CX, CZ = NC * PER, NC * PER + 3
 NSEM = NC * PER + 6
 
 SCHEDULE = (
-    "ta:0", "s0:0", "tc:0", "tb:2", "tc:2", "s0:1", "ta:2", "s0:2", "tb:0", "s1:0", "s2:0",
-    "s2:1", "tb:4", "tc:4", "s1:1", "s2:2", "td:0", "s1:2", "ta:4", "s0:3", "s3:0", "prepare",
-    "s3:1", "s0:4", "td:2", "s3:2", "s0:5", "s2:3", "s1:3", "s2:4", "s4:0", "s4:1", "s1:4",
-    "s1:5", "s4:2", "s3:3", "s2:5", "td:4", "s3:4", "s3:5", "s5:0", "s5:1", "s6:1", "s6:0",
-    "s5:2", "peaks:0", "peaks:1", "s4:3", "s6:2", "s4:4", "s7:1", "s7:0", "s4:5", "peaks:2",
-    "s7:2", "s5:3", "s5:4", "peaks:3", "s6:3", "s8:0", "peaks:4", "s6:4", "s8:1", "s5:5",
-    "peaks:5", "s8:2", "s6:5", "s7:3", "s7:4", "s7:5", "u0", "s8:3", "s9:0", "s8:4", "s9:1",
-    "s8:5", "s9:2", "s10:0", "t1:2", "s10:1", "s10:2", "t1:3", "t1:4", "t1:1", "s9:3", "s9:4",
-    "s11:0", "s11:1", "u1", "s9:5", "s11:2", "t2:4", "s10:3", "s12:0", "t2:1", "s10:4", "s10:5",
-    "pa:4", "s12:1", "t1:0", "s12:2", "s11:3", "t2:3", "t2:2", "t1:5", "s11:4", "both:0",
-    "s11:5", "pa:5", "u2", "s12:3", "pb:4", "t2:0", "t2:5", "s12:4", "pb:5", "s12:5", "both:2",
-    "pc:4", "pc:5",
+    "ta:0", "s0:0:0", "ta:4", "s0:4:0", "tc:0", "tb:0", "s1:0:0", "s0:5:0", "tc:4", "ta:2",
+    "s2:0:0", "s0:1:0", "tb:4", "s1:4:0", "td:4", "s2:4:0", "s1:5:0", "s0:0:1", "td:0",
+    "s3:0:0", "s2:5:0", "s0:5:1", "s2:1:0", "s3:4:0", "prepare", "s0:4:1", "s1:1:0", "s0:2:0",
+    "s0:3:0", "s2:0:1", "s3:5:0", "s1:0:1", "s2:5:1", "s1:5:1", "s1:4:1", "s3:1:0", "s0:1:1",
+    "tb:2", "s2:4:1", "tc:2", "s2:2:0", "s3:0:1", "s4:0", "s1:2:0", "s0:2:1", "s3:5:1", "s4:5",
+    "s2:3:0", "td:2", "s1:3:0", "s3:4:1", "s4:4", "s1:1:1", "s3:2:0", "s0:3:1", "s2:1:1",
+    "s2:2:1", "s1:2:1", "s3:3:0", "s1:3:1", "s2:3:1", "s3:1:1", "s4:1", "s5:0", "s3:2:1",
+    "s4:2", "s5:5", "s5:4", "s3:3:1", "s7:0", "s4:3", "s7:4", "s5:1", "s7:5", "s8:0", "peaks:0",
+    "peaks:1", "s5:2", "s5:3", "peaks:5", "s8:4", "peaks:4", "s7:1", "s8:5", "s7:2", "s7:3",
+    "s9:0", "peaks:3", "s8:1", "peaks:2", "u0", "s8:2", "s9:4", "s8:3", "u1", "s10:0", "t1:0",
+    "s9:5", "t1:1", "s10:4", "s9:1", "s9:2", "s11:0", "s10:5", "t1:4", "t1:2", "t1:3", "s9:3",
+    "s11:4", "t1:5", "t2:2", "s10:1", "s10:2", "t2:3", "pa:4", "t2:1", "pa:0", "s12:4", "s10:3",
+    "s11:5", "t2:0", "t2:4", "t2:5", "s11:1", "s12:0", "u2", "s11:2", "pb:4", "s11:3", "pa:2",
+    "pb:0", "s12:5", "s12:1", "s12:2", "s12:3", "pb:2", "pc:4", "pc:0", "pc:2",
 )
 
 
@@ -57,7 +58,7 @@
     nw_h, nm_h, fs_h, ss_h, frmo_h, fcmo_h, srmo_h, scmo_h, keys_h,
     tok, cot, wgt, omom, codes, frm, fcm, srm, scm, insem,
     nw_o, nm_o, fs_o, ss_o, frm_o, fcm_o, srm_o, scm_o, keys_o, outsem,
-    term, xr, cbuf, zf, zs, zr, zc, pf, pcs, pcr, ysf, ysb, yr, zlb, avgt, wbuf, acc,
+    term, xr, cbuf, zf, zs, zr, zc, pf, pcs, yr, zlb, avgt, wbuf, acc,
     wf, rows, rmax, cmx, cmz, fnew, snew, ssem, rsem,
 ):
     x, zh = lax.axis_index("x"), lax.axis_index("zh")
@@ -73,31 +74,45 @@
     oc = 1 - c
     partner = {"core": oc}
 
-    barrier = pltpu.get_barrier_semaphore()
-    for axis in ("zh", "zl", "y", "x"):
-        for o in (2, 1, 3):
-            pl.semaphore_signal(barrier, inc=1, device_id=to(axis, o), device_id_type=MESH)
-    pl.semaphore_signal(barrier, inc=1, device_id=partner, device_id_type=MESH)
+    near = (at("zh", 2), at("zh", 1), at("zh", -1), zh)
+    owners = (at("x", 2), at("x", 1), at("x", -1), x)
 
     def token_columns(owner):
         return pl.ds(pl.multiple_of(owner * 512, 512), 512)
 
-    def token_copy(n, owner):
-        cols = token_columns(owner)
-        return pltpu.make_async_copy(tok_h.at[0, :, cols], tok.at[0, :, cols], insem.at[n])
-
-    owners = (at("x", 2), at("x", 1), at("x", -1), x)
-    cot_copy = pltpu.make_async_copy(cot_h, cot, insem.at[4])
+    def token_copies(slot):
+        copies = []
+        for r in range(4):
+            src = pl.ds(pl.multiple_of(owners[slot] * 512 + near[r] * T, T), T)
+            dst = pl.ds(pl.multiple_of(owners[slot] * 512 + r * T, T), T)
+            copies.append(pltpu.make_async_copy(
+                tok_h.at[0, :, src], tok.at[0, :, dst], insem.at[4 * slot + r]
+            ))
+        return copies
+
+    cot_copy = pltpu.make_async_copy(cot_h, cot, insem.at[16])
     small_copies = [
-        pltpu.make_async_copy(src, dst, insem.at[5 + n])
+        pltpu.make_async_copy(src, dst, insem.at[17 + n])
         for n, (src, dst) in enumerate((
             (codes_h, codes), (wgt_h, wgt), (omom_h, omom),
             (frm_h, frm), (fcm_h, fcm), (srm_h, srm), (scm_h, scm),
         ))
     ]
     cot_copy.start()
-    for n in range(4):
-        token_copy(n, owners[n]).start()
+    for copy in token_copies(0):
+        copy.start()
+
+    barrier = pltpu.get_barrier_semaphore()
+    far_copy = {"zh": at("zh", 2), "zl": at("zl", 2)}
+    partners = [to(axis, o) for axis in ("zh", "zl", "y", "x") for o in (2, 1, 3)]
+    partners += [far_copy, partner]
+    partners += [{"y": at("y", o), "core": oc} for o in (2, 1, 3)]
+    for device in partners:
+        pl.semaphore_signal(barrier, inc=1, device_id=device, device_id_type=MESH)
+
+    for slot in (1, 2, 3):
+        for copy in token_copies(slot):
+            copy.start()
     for copy in small_copies:
         copy.start()
 
@@ -135,10 +150,11 @@
             (((0,), (0,)), ((), ())), preferred_element_type=f32,
         ).astype(bf16)
         for n in range(count):
-            for block in range(4):
+            for r in range(4):
                 for ab in (0, 1):
-                    r = block * T + ab * H
-                    term[first + n, slot, ab, block] = part[r:r + H, columns(n)]
+                    start = (0, 2, 1, 3)[r] if ab else r
+                    start = start * T + ab * H
+                    term[first + n, slot, ab, r] = part[start:start + H, columns(n)]
 
     loaded = set()
 
@@ -146,7 +162,8 @@
         if not loaded:
             cot_copy.wait()
         if slot not in loaded:
-            token_copy(slot, owners[slot]).wait()
+            for copy in token_copies(slot):
+                copy.wait()
             loaded.add(slot)
         terms(slot, k, 2)
 
@@ -169,60 +186,60 @@
         rows[0] = jnp.broadcast_to(frm[...], (T, T)).T
         rows[1] = jnp.broadcast_to(srm[...], (T, T)).T
 
-    def s0(k):
-        b = k * PER
-        if k == 0:
-            pl.semaphore_wait(barrier, 13)
-        send(b + XF, term.at[k, 0, 0], xr.at[k, 0, 0], to("x", -1))
-        send(b + XF + 1, term.at[k, 0, 1], xr.at[k, 0, 1], to("x", 1))
-
-    def s1(k):
-        b = k * PER
-        send(b + XD, term.at[k, 1, 0], xr.at[k, 1, 0], to("x", 1))
-        send(b + XD + 1, term.at[k, 2, 1], xr.at[k, 1, 1], to("x", -1))
-
-    def s2(k):
-        b = k * PER
+    def halves(ref, h):
+        return ref.at[2 * h:2 * h + 2]
+
+    def s0(k, h):
+        b = k * PER + XF + 2 * h
+        if k == 0 and h == 0:
+            pl.semaphore_wait(barrier, len(partners))
+        for ab, way in ((0, -1), (1, 1)):
+            send(b + ab, halves(term.at[k, 0, ab], h), halves(xr.at[k, 0, ab], h), to("x", way))
+
+    def s1(k, h):
+        b = k * PER + XD + 2 * h
+        for ab, slot, way in ((0, 1, 1), (1, 2, -1)):
+            send(b + ab, halves(term.at[k, slot, ab], h), halves(xr.at[k, 1, ab], h), to("x", way))
+
+    def s2(k, h):
+        b = k * PER + 2 * h
+        part = slice(2 * h, 2 * h + 2)
         for ab, slot, way in ((0, 2, -1), (1, 1, 1)):
-            arrived(b + XF + ab, xr.at[k, 0, ab])
-            cbuf[k, ab] = (term[k, slot, ab].astype(f32) + xr[k, 0, ab].astype(f32)).astype(bf16)
-            send(b + XC + ab, cbuf.at[k, ab], xr.at[k, 2, ab], to("x", way))
-
-    def s3(k):
-        b = k * PER
+            arrived(b + XF + ab, halves(xr.at[k, 0, ab], h))
+            cbuf[k, ab, part] = (
+                term[k, slot, ab, part].astype(f32) + xr[k, 0, ab, part].astype(f32)
+            ).astype(bf16)
+            send(b + XC + ab, halves(cbuf.at[k, ab], h), halves(xr.at[k, 2, ab], h), to("x", way))
+
+    def s3(k, h):
+        b = k * PER + 2 * h
+        part = slice(2 * h, 2 * h + 2)
         for ab in (0, 1):
-            arrived(b + XD + ab, xr.at[k, 1, ab])
+            arrived(b + XD + ab, halves(xr.at[k, 1, ab], h))
         for ab in (0, 1):
-            arrived(b + XC + ab, xr.at[k, 2, ab])
-
-        def total(ab, block):
+            arrived(b + XC + ab, halves(xr.at[k, 2, ab], h))
+        for ab in (0, 1):
             value = (
-                term[k, 3, ab, block].astype(f32)
-                + xr[k, 1, ab, block].astype(f32)
-                + xr[k, 2, ab, block].astype(f32)
+                term[k, 3, ab, part].astype(f32)
+                + xr[k, 1, ab, part].astype(f32)
+                + xr[k, 2, ab, part].astype(f32)
             )
-            zf[k, ab, block] = value
-            zs[k, ab, block] = value.astype(bf16)
-
-        far, after, before = at("zh", 2), at("zh", 1), at("zh", -1)
-        total(0, far)
-        send(b + ZF, zs.at[k, 0, far], zr.at[k, 0, 0], to("zh", -1))
-        total(1, far)
-        send(b + ZF + 1, zs.at[k, 1, far], zr.at[k, 0, 1], to("zh", 1))
-        total(0, after)
-        send(b + ZD, zs.at[k, 0, after], zr.at[k, 1, 0], to("zh", 1))
-        total(1, before)
-        send(b + ZD + 1, zs.at[k, 1, before], zr.at[k, 1, 1], to("zh", -1))
-        total(1, after)
-        total(0, before)
-        total(0, zh)
-        total(1, zh)
+            if h == 0:
+                zs[k, ab] = value.astype(bf16)
+            else:
+                zf[k, ab] = value
+        if h == 0:
+            b = k * PER
+            send(b + ZF, zs.at[k, 0, 0], zr.at[k, 0, 0], to("zh", -1))
+            send(b + ZF + 1, zs.at[k, 1, 0], zr.at[k, 0, 1], to("zh", 1))
+            send(b + ZD, zs.at[k, 0, 1], zr.at[k, 1, 0], to("zh", 1))
+            send(b + ZD + 1, zs.at[k, 1, 1], zr.at[k, 1, 1], to("zh", -1))
 
     def s4(k):
         b = k * PER
         for ab, way in ((0, -1), (1, 1)):
             arrived(b + ZF + ab, zr.at[k, 0, ab])
-            zc[k, ab] = (zf[k, ab, at("zh", way)] + zr[k, 0, ab].astype(f32)).astype(bf16)
+            zc[k, ab] = (zf[k, ab, 0] + zr[k, 0, ab].astype(f32)).astype(bf16)
             send(b + ZC + ab, zc.at[k, ab], zr.at[k, 2, ab], to("zh", way))
 
     def s5(k):
@@ -234,7 +251,7 @@
         cols = columns(k)
         for ab in (0, 1):
             half = slice(ab * H, (ab + 1) * H)
-            gradient = zf[k, ab, zh] + zr[k, 1, ab].astype(f32) + zr[k, 2, ab].astype(f32)
+            gradient = zf[k, ab, 1] + zr[k, 1, ab].astype(f32) + zr[k, 2, ab].astype(f32)
             packed = codes[0, half, cols]
             first_code = (packed >> 4).astype(f32)
             second_code = (packed & 15).astype(f32)
@@ -247,8 +264,13 @@
             pf[k, ab] = inner_rate * (update + weight_decay * wf[half, cols])
             fnew[half, cols] = first_new
             snew[half, cols] = second_new
-        pcs[k] = pf[k, oc].astype(bf16)
-        send(b + CE, pcs.at[k], pcr.at[k], partner)
+            pcs[k, ab] = pf[k, ab].astype(bf16)
+        for o in (2, 1, 3, 0):
+            theirs = rows_of(at("y", o) * Q, Q)
+            for other in ((1,) if o == 0 else (0, 1)):
+                device = {"y": at("y", o), "core": oc if other else c}
+                slot = o + 3 * other - 1 if o else 6
+                send(b + YS + slot, pcs.at[k, device["core"], theirs, :], yr.at[k, slot], device)
 
     def peaks(k):
         cols = columns(k)
@@ -256,16 +278,6 @@
             cmx[x, m:m + 1, cols] = jnp.max(value, axis=0, keepdims=True)
             rmax[m] = value if k == 0 else jnp.maximum(rmax[m], value)
 
-    def s6(k):
-        b = k * PER
-        arrived(b + CE, pcr.at[k])
-        both = pf[k, c] + pcr[k].astype(f32)
-        ysf[k] = both
-        ysb[k] = both.astype(bf16)
-        for o in (2, 1, 3):
-            theirs = rows_of(at("y", o) * Q, Q)
-            send(b + YS + o - 1, ysb.at[k, theirs, :], yr.at[k, o - 1], to("y", o))
-
     mine = rows_of(y * Q, Q)
     mine_of_block = rows_of(c * H + y * Q, Q)
     my_half = rows_of(c * H, H)
@@ -273,12 +285,12 @@
 
     def s7(k):
         b = k * PER
-        for o in (1, 2, 3):
-            arrived(b + YS + o - 1, yr.at[k, o - 1])
-        zlb[k, zl] = (
-            ysf[k, mine, :]
-            + yr[k, 0].astype(f32) + yr[k, 1].astype(f32) + yr[k, 2].astype(f32)
-        ).astype(bf16)
+        for slot in range(7):
+            arrived(b + YS + slot, yr.at[k, slot])
+        total = pf[k, c, mine, :]
+        for slot in range(7):
+            total = total + yr[k, slot].astype(f32)
+        zlb[k, zl] = total.astype(bf16)
         for o in (1, 2, 3):
             send(b + LS + o - 1, zlb.at[k, zl], zlb.at[k, zl], to("zl", o))
 
@@ -294,7 +306,7 @@
         wbuf[k, x, zh, mine_of_block, :] = weights.astype(bf16)
         for o in (2, 1, 3):
             piece = wbuf.at[k, x, zh, mine_of_block, :]
-            send(b + HS + o - 1, piece, piece, to("zh", o))
+            send(b + HS + o - 1, piece, piece, far_copy if o == 2 else to("zh", o))
         avgt[k, mine_of_block, :] = averaged
         for o in (1, 2, 3):
             piece = avgt.at[k, mine_of_block, :]
@@ -346,38 +358,22 @@
         arrived(k * PER + WC + n, wbuf.at[k, at_x, :, other_half, :])
 
     def block_of(k, at_x):
-        return wbuf[k, at_x].reshape(512, T)
+        return jnp.concatenate([wbuf[k, at_x, block] for block in near], axis=0)
 
     places = (x, at("x", -1), at("x", 1), at("x", 2))
 
-    def product(k, count):
-        for n in range(count):
-            for i in range(4):
-                from_partner(k + n, i, places[i])
-        total = None
-        for at_x in range(4):
-            rhs = jnp.concatenate([block_of(k + n, at_x) for n in range(count)], axis=1)
-            part = jnp.dot(tok[0, :, at_x * 512:(at_x + 1) * 512], rhs, preferred_element_type=f32)
-            total = part if total is None else total + part
-        keys_o[0, :, columns(k, count)] = total.astype(bf16)
-        leave(keys_o.at[0, :, columns(k, count)], keys_h.at[0, :, columns(k, count)])
-
-    def both(k):
-        product(k, 2)
-
     def partial(k, i):
-        from_partner(k, i, places[i])
-        part = jnp.dot(
-            tok[0, :, token_columns(places[i])], block_of(k, places[i]),
-            preferred_element_type=f32,
-        )
+        for n in (0, 1):
+            from_partner(k + n, i, places[i])
+        rhs = jnp.concatenate([block_of(k + n, places[i]) for n in (0, 1)], axis=1)
+        part = jnp.dot(tok[0, :, token_columns(places[i])], rhs, preferred_element_type=f32)
         if i > 0:
-            part = part + acc[k - NC + 2]
+            part = part + acc[k // 2]
         if i < 3:
-            acc[k - NC + 2] = part
+            acc[k // 2] = part
         else:
-            keys_o[0, :, columns(k)] = part.astype(bf16)
-            leave(keys_o.at[0, :, columns(k)], keys_h.at[0, :, columns(k)])
+            keys_o[0, :, columns(k, 2)] = part.astype(bf16)
+            leave(keys_o.at[0, :, columns(k, 2)], keys_h.at[0, :, columns(k, 2)])
 
     def pa(k):
         partial(k, 0)
@@ -444,8 +440,8 @@
     stages = {
         f.__name__: f
         for f in (
-            ta, tb, tc, td, prepare, s0, s1, s2, s3, s4, s5, peaks, s6, s7, s8, s9, s10, s11, s12,
-            both, pa, pb, pc, t1, t2, u0, u1, u2,
+            ta, tb, tc, td, prepare, s0, s1, s2, s3, s4, s5, peaks, s7, s8, s9, s10, s11, s12,
+            pa, pb, pc, t1, t2, u0, u1, u2,
         )
     }
     for entry in SCHEDULE:
@@ -490,26 +486,23 @@
         out_specs=(hbm,) * 9,
         scratch_shapes=[
             *(pltpu.VMEM(a.shape, a.dtype) for a in arguments),
-            pltpu.SemaphoreType.DMA((12,)),
+            pltpu.SemaphoreType.DMA((24,)),
             *(pltpu.VMEM(a.shape, a.dtype) for a in outs),
             pltpu.SemaphoreType.DMA((16,)),
             pltpu.VMEM((NC, 4, 2, 4, H, T), bf16),
             pltpu.VMEM((NC, 3, 2, 4, H, T), bf16),
             pltpu.VMEM((NC, 2, 4, H, T), bf16),
-            pltpu.VMEM((NC, 2, 4, H, T), f32),
-            pltpu.VMEM((NC, 2, 4, H, T), bf16),
+            pltpu.VMEM((NC, 2, 2, H, T), f32),
+            pltpu.VMEM((NC, 2, 2, H, T), bf16),
             pltpu.VMEM((NC, 3, 2, H, T), bf16),
             pltpu.VMEM((NC, 2, H, T), bf16),
             pltpu.VMEM((NC, 2, H, T), f32),
-            pltpu.VMEM((NC, H, T), bf16),
-            pltpu.VMEM((NC, H, T), bf16),
-            pltpu.VMEM((NC, H, T), f32),
-            pltpu.VMEM((NC, H, T), bf16),
-            pltpu.VMEM((NC, 3, Q, T), bf16),
+            pltpu.VMEM((NC, 2, H, T), bf16),
+            pltpu.VMEM((NC, 7, Q, T), bf16),
             pltpu.VMEM((NC, 4, Q, T), bf16),
             pltpu.VMEM((NC, T, T), f32),
             pltpu.VMEM((NC, 4, 4, T, T), bf16),
-            pltpu.VMEM((2, 512, T), f32),
+            pltpu.VMEM((NC // 2, 512, 2 * T), f32),
             pltpu.VMEM((T, 768), f32),
             pltpu.VMEM((2, T, T), f32),
             pltpu.VMEM((2, T, T), f32),

time: 93.7 us -> 89.8 us (0.958)
  Pallas kernels: 92.9 us -> 88.9 us
    pallas_call x1, Pallas kernels: 90.4 us -> 86.4 us  [local(): pl.pallas_call(kernel, out_shape=outs, in_specs=[hbm] * 9, out_specs=(hbm...]
where the time goes in v3:
time: 89.8 us; the launch traced here: 89.6 us
  Pallas kernels  88.9 us (99%)
    pallas_call x1, Pallas kernels, local(): pl.pallas_call(kernel, out_shape=outs, in_specs=[hbm] * 9, out_specs=(hbm...  86.4 us
    pallas_call x1, Pallas kernels, local(): pl.pallas_call(deliver, out_shape=outs, in_specs=[hbm] * 9, out_specs=(hb...  2.56 us

profile of v3, /device:TPU:1, one launch (start us, length us, event | category | flops | bytes accessed | tf_op | source)
XLA Modules:
  0.0 89.6 jit_solution(13982859330140189802)
XLA Ops:
  0.6 86.4 %round.1 = (f32[128,768]{1,0:T(8,128)}, f32[128,768]{1,0:T(8,128)}, bf16[1,128,768]{2,1,0:T(8,128)(2,1)}, bf16[1,128,768]{2,1,0:T(8,128)(2,1)}, f32[1,128]{1,0:T...) custom-call(bf16[1,512,2048]{2,1,0:T(8,128)(2,1)} %tok_h.1, ...), custom_call_target="tpu_custom_call" | custom-call | tf_op jit(solution)/shard_map/round/pallas_call | solution.py:482
  87.0 2.6 %deliver.1 = (f32[128,768]{1,0:T(8,128)}, f32[128,768]{1,0:T(8,128)}, bf16[1,128,768]{2,1,0:T(8,128)(2,1)}, bf16[1,128,768]{2,1,0:T(8,128)(2,1)}, f32[1,128]{1,0...) custom-call(f32[128,768]{1,0:T(8,128)} %get-tuple-element.18.refs_0_, ...), custom_call_target="tpu_custom_call" | custom-call | tf_op jit(solution)/shard_map/deliver/pallas_call | solution.py:521

commit v4 on v3

--- a/solution.py
+++ b/solution.py
@@ -30,26 +30,27 @@
 
 XF, XD, XC, ZF, ZD, ZC = 0, 4, 8, 12, 14, 16
 YS, LS, HS, AY, WY = 18, 25, 28, 31, 34
-WX, WF, WC, AC = 37, 39, 41, 45
-PER = 46
+WX, WF, WC, AC = 37, 41, 43, 47
+PER = 48
 CX, CZ = NC * PER, NC * PER + 3
 NSEM = NC * PER + 6
 
 SCHEDULE = (
-    "ta:0", "s0:0:0", "ta:4", "s0:4:0", "tc:0", "tb:0", "s1:0:0", "s0:5:0", "tc:4", "ta:2",
-    "s2:0:0", "s0:1:0", "tb:4", "s1:4:0", "td:4", "s2:4:0", "s1:5:0", "s0:0:1", "td:0",
-    "s3:0:0", "s2:5:0", "s0:5:1", "s2:1:0", "s3:4:0", "prepare", "s0:4:1", "s1:1:0", "s0:2:0",
-    "s0:3:0", "s2:0:1", "s3:5:0", "s1:0:1", "s2:5:1", "s1:5:1", "s1:4:1", "s3:1:0", "s0:1:1",
-    "tb:2", "s2:4:1", "tc:2", "s2:2:0", "s3:0:1", "s4:0", "s1:2:0", "s0:2:1", "s3:5:1", "s4:5",
-    "s2:3:0", "td:2", "s1:3:0", "s3:4:1", "s4:4", "s1:1:1", "s3:2:0", "s0:3:1", "s2:1:1",
-    "s2:2:1", "s1:2:1", "s3:3:0", "s1:3:1", "s2:3:1", "s3:1:1", "s4:1", "s5:0", "s3:2:1",
-    "s4:2", "s5:5", "s5:4", "s3:3:1", "s7:0", "s4:3", "s7:4", "s5:1", "s7:5", "s8:0", "peaks:0",
-    "peaks:1", "s5:2", "s5:3", "peaks:5", "s8:4", "peaks:4", "s7:1", "s8:5", "s7:2", "s7:3",
-    "s9:0", "peaks:3", "s8:1", "peaks:2", "u0", "s8:2", "s9:4", "s8:3", "u1", "s10:0", "t1:0",
-    "s9:5", "t1:1", "s10:4", "s9:1", "s9:2", "s11:0", "s10:5", "t1:4", "t1:2", "t1:3", "s9:3",
-    "s11:4", "t1:5", "t2:2", "s10:1", "s10:2", "t2:3", "pa:4", "t2:1", "pa:0", "s12:4", "s10:3",
-    "s11:5", "t2:0", "t2:4", "t2:5", "s11:1", "s12:0", "u2", "s11:2", "pb:4", "s11:3", "pa:2",
-    "pb:0", "s12:5", "s12:1", "s12:2", "s12:3", "pb:2", "pc:4", "pc:0", "pc:2",
+    "ta:0", "s0:0:0", "tb:0", "s0:1:0", "tc:0", "s1:0:0", "td:4", "s1:1:0", "ta:4", "s2:0:0",
+    "ta:2", "s0:3:0", "s0:2:0", "tc:2", "tb:2", "s2:1:0", "s1:3:0", "td:0", "s0:0:1", "tc:4",
+    "s3:0:0", "s2:3:0", "s1:2:0", "s0:1:1", "s2:2:0", "s0:3:1", "td:2", "s1:0:1", "s3:1:0",
+    "s2:0:1", "s0:5:0", "s1:1:1", "s3:3:0", "s0:2:1", "s2:1:1", "s0:4:0", "s2:3:1", "s3:2:0",
+    "tb:4", "s3:0:1", "s1:3:1", "prepare", "s2:5:0", "s1:5:0", "s4:0", "s0:5:1", "s2:4:0",
+    "s3:1:1", "s4:1", "s1:2:1", "s1:4:0", "s3:3:1", "s4:3", "s3:5:0", "s0:4:1", "s2:2:1",
+    "s2:5:1", "s3:4:0", "s5:0", "peaks:0", "s1:5:1", "s2:4:1", "s1:4:1", "s5:3", "s3:2:1",
+    "s4:2", "s5:1", "peaks:1", "s3:5:1", "s4:5", "s7:0", "s3:4:1", "s4:4", "s7:1", "s7:3",
+    "s5:2", "peaks:2", "s8:0", "s5:5", "s8:1", "s5:4", "s8:3", "s7:2", "s7:5", "t1:1",
+    "peaks:4", "peaks:5", "t1:0", "peaks:3", "u0", "s9:0", "s7:4", "s8:2", "t1:3", "s9:1",
+    "s8:5", "s9:3", "s8:4", "s10:0", "s10:1", "u1", "t1:2", "t1:5", "s9:2", "s10:3", "s9:5",
+    "pa:0", "s11:0", "s11:1", "s9:4", "s11:3", "t1:4", "v11:1", "v11:0", "t2:0", "s10:2",
+    "s10:5", "s10:4", "pa:2", "v11:3", "pb:0", "s11:2", "s12:1", "s11:5", "v11:2", "s12:0",
+    "s12:3", "s11:4", "t2:3", "t2:4", "t2:1", "v11:5", "u2", "t2:2", "t2:5", "pc:0", "v11:4",
+    "s12:2", "pb:2", "s12:4", "s12:5", "pa:4", "pb:4", "pc:2", "pc:4",
 )
 
 
@@ -104,8 +105,9 @@
 
     barrier = pltpu.get_barrier_semaphore()
     far_copy = {"zh": at("zh", 2), "zl": at("zl", 2)}
-    partners = [to(axis, o) for axis in ("zh", "zl", "y", "x") for o in (2, 1, 3)]
-    partners += [far_copy, partner]
+    partners = [to("zh", 1), to("zh", 3), to("x", 1), to("x", 3)]
+    partners += [to(axis, o) for axis in ("zl", "y") for o in (2, 1, 3)]
+    partners += [partner]
     partners += [{"y": at("y", o), "core": oc} for o in (2, 1, 3)]
     for device in partners:
         pl.semaphore_signal(barrier, inc=1, device_id=device, device_id_type=MESH)
@@ -328,20 +330,28 @@
         for o in (1, 2, 3):
             theirs = rows_of(c * H + at("y", -o) * Q, Q)
             arrived(b + WY + o - 1, wbuf.at[k, x, :, theirs, :])
+        first, second = half_block(k, x, slice(0, 2)), half_block(k, x, slice(2, 4))
+        send(b + WX, first, first, to("x", 1))
+        send(b + WX + 1, second, second, to("x", -1))
+        send(b + WX + 2, second, second, to("x", 1))
+        send(b + WX + 3, first, first, to("x", -1))
         block = half_block(k, x)
-        send(b + WX, block, block, to("x", 1))
-        send(b + WX + 1, block, block, to("x", -1))
         send(b + WC, block, block, partner)
 
     def s11(k):
         b = k * PER
+        part = half_block(k, at("x", -1), slice(0, 2))
+        arrived(b + WX, part)
+        send(b + WF, part, part, to("x", 1))
+        part = half_block(k, at("x", 1), slice(2, 4))
+        arrived(b + WX + 1, part)
+        send(b + WF + 1, part, part, to("x", -1))
+
+    def v11(k):
+        b = k * PER
         before, after = at("x", -1), at("x", 1)
-        arrived(b + WX, half_block(k, before))
-        part = half_block(k, before, slice(0, 2))
-        send(b + WF, part, part, to("x", 1))
-        arrived(b + WX + 1, half_block(k, after))
-        part = half_block(k, after, slice(2, 4))
-        send(b + WF + 1, part, part, to("x", -1))
+        arrived(b + WX + 2, half_block(k, before, slice(2, 4)))
+        arrived(b + WX + 3, half_block(k, after, slice(0, 2)))
         for n, at_x in ((1, before), (2, after)):
             block = half_block(k, at_x)
             send(b + WC + n, block, block, partner)
@@ -440,7 +450,7 @@
     stages = {
         f.__name__: f
         for f in (
-            ta, tb, tc, td, prepare, s0, s1, s2, s3, s4, s5, peaks, s7, s8, s9, s10, s11, s12,
+            ta, tb, tc, td, prepare, s0, s1, s2, s3, s4, s5, peaks, s7, s8, s9, s10, s11, v11, s12,
             pa, pb, pc, t1, t2, u0, u1, u2,
         )
     }

time: 89.8 us -> 86.5 us (0.963)
  Pallas kernels: 88.9 us -> 85.7 us
    pallas_call x1, Pallas kernels: 86.4 us -> 83.2 us  [local(): pl.pallas_call(kernel, out_shape=outs, in_specs=[hbm] * 9, out_specs=(hbm...]
where the time goes in v4:
time: 86.5 us; the launch traced here: 86.4 us
  Pallas kernels  85.7 us (99%)
    pallas_call x1, Pallas kernels, local(): pl.pallas_call(kernel, out_shape=outs, in_specs=[hbm] * 9, out_specs=(hbm...  83.2 us
    pallas_call x1, Pallas kernels, local(): pl.pallas_call(deliver, out_shape=outs, in_specs=[hbm] * 9, out_specs=(hb...  2.56 us

profile of v4, /device:TPU:1, one launch (start us, length us, event | category | flops | bytes accessed | tf_op | source)
XLA Modules:
  0.0 86.4 jit_solution(13974747989542877030)
XLA Ops:
  0.6 83.2 %round.1 = (f32[128,768]{1,0:T(8,128)}, f32[128,768]{1,0:T(8,128)}, bf16[1,128,768]{2,1,0:T(8,128)(2,1)}, bf16[1,128,768]{2,1,0:T(8,128)(2,1)}, f32[1,128]{1,0:T...) custom-call(bf16[1,512,2048]{2,1,0:T(8,128)(2,1)} %tok_h.1, ...), custom_call_target="tpu_custom_call" | custom-call | tf_op jit(solution)/shard_map/round/pallas_call | solution.py:492
  83.8 2.6 %deliver.1 = (f32[128,768]{1,0:T(8,128)}, f32[128,768]{1,0:T(8,128)}, bf16[1,128,768]{2,1,0:T(8,128)(2,1)}, bf16[1,128,768]{2,1,0:T(8,128)(2,1)}, f32[1,128]{1,0...) custom-call(f32[128,768]{1,0:T(8,128)} %get-tuple-element.18.refs_0_, ...), custom_call_target="tpu_custom_call" | custom-call | tf_op jit(solution)/shard_map/deliver/pallas_call | solution.py:531

commit v5 on v4

--- a/solution.py
+++ b/solution.py
@@ -33,7 +33,20 @@
 WX, WF, WC, AC = 37, 41, 43, 47
 PER = 48
 CX, CZ = NC * PER, NC * PER + 3
-NSEM = NC * PER + 6
+GROUPS_OF = (
+    0, 0, 1, 1, 2, 2, 3, 3, 2, 2, 3, 3, 4, 4, 5, 5, 5, 5, 6, 6, 6, 6, 6, 6, 6, 7, 7, 7, 8, 8, 8,
+    9, 9, 9, 10, 10, 10, 11, 12, 13, 13, 14, 14, 15, 16, 17, 18, 19,
+)
+PER_SEM = 20
+NRECV = NC * PER_SEM + 2
+NSEND = 64
+
+
+def receive_semaphore(number):
+    if number >= CX:
+        return NC * PER_SEM + (number >= CZ)
+    return number // PER * PER_SEM + GROUPS_OF[number % PER]
+
 
 SCHEDULE = (
     "ta:0", "s0:0:0", "tb:0", "s0:1:0", "tc:0", "s1:0:0", "td:4", "s1:1:0", "ta:4", "s2:0:0",
@@ -87,13 +100,13 @@
             src = pl.ds(pl.multiple_of(owners[slot] * 512 + near[r] * T, T), T)
             dst = pl.ds(pl.multiple_of(owners[slot] * 512 + r * T, T), T)
             copies.append(pltpu.make_async_copy(
-                tok_h.at[0, :, src], tok.at[0, :, dst], insem.at[4 * slot + r]
+                tok_h.at[0, :, src], tok.at[0, :, dst], insem.at[slot]
             ))
         return copies
 
-    cot_copy = pltpu.make_async_copy(cot_h, cot, insem.at[16])
+    cot_copy = pltpu.make_async_copy(cot_h, cot, insem.at[4])
     small_copies = [
-        pltpu.make_async_copy(src, dst, insem.at[17 + n])
+        pltpu.make_async_copy(src, dst, insem.at[5 + n])
         for n, (src, dst) in enumerate((
             (codes_h, codes), (wgt_h, wgt), (omom_h, omom),
             (frm_h, frm), (fcm_h, fcm), (srm_h, srm), (scm_h, scm),
@@ -121,8 +134,12 @@
     started, leaving = [], []
 
     def send(number, src, dst, device):
+        index = len(started) % NSEND
+        if len(started) >= NSEND:
+            started[-NSEND].wait_send()
         copy = pltpu.make_async_remote_copy(
-            src_ref=src, dst_ref=dst, send_sem=ssem.at[number], recv_sem=rsem.at[number],
+            src_ref=src, dst_ref=dst, send_sem=ssem.at[index],
+            recv_sem=rsem.at[receive_semaphore(number)],
             device_id=device, device_id_type=MESH,
         )
         copy.start()
@@ -130,8 +147,8 @@
 
     def arrived(number, dst):
         pltpu.make_async_remote_copy(
-            src_ref=dst, dst_ref=dst, send_sem=ssem.at[number], recv_sem=rsem.at[number],
-            device_id=partner, device_id_type=MESH,
+            src_ref=dst, dst_ref=dst, send_sem=ssem.at[0],
+            recv_sem=rsem.at[receive_semaphore(number)], device_id=partner, device_id_type=MESH,
         ).wait_recv()
 
     def leave(src, dst):
@@ -164,8 +181,8 @@
         if not loaded:
             cot_copy.wait()
         if slot not in loaded:
-            for copy in token_copies(slot):
-                copy.wait()
+            cols = token_columns(owners[slot])
+            pltpu.make_async_copy(tok_h.at[0, :, cols], tok.at[0, :, cols], insem.at[slot]).wait()
             loaded.add(slot)
         terms(slot, k, 2)
 
@@ -206,8 +223,8 @@
     def s2(k, h):
         b = k * PER + 2 * h
         part = slice(2 * h, 2 * h + 2)
+        arrived(b + XF, xr.at[k, 0, :, part])
         for ab, slot, way in ((0, 2, -1), (1, 1, 1)):
-            arrived(b + XF + ab, halves(xr.at[k, 0, ab], h))
             cbuf[k, ab, part] = (
                 term[k, slot, ab, part].astype(f32) + xr[k, 0, ab, part].astype(f32)
             ).astype(bf16)
@@ -216,10 +233,7 @@
     def s3(k, h):
         b = k * PER + 2 * h
         part = slice(2 * h, 2 * h + 2)
-        for ab in (0, 1):
-            arrived(b + XD + ab, halves(xr.at[k, 1, ab], h))
-        for ab in (0, 1):
-            arrived(b + XC + ab, halves(xr.at[k, 2, ab], h))
+        arrived(b + XD, xr.at[k, 1:3, :, part])
         for ab in (0, 1):
             value = (
                 term[k, 3, ab, part].astype(f32)
@@ -239,17 +253,14 @@
 
     def s4(k):
         b = k * PER
+        arrived(b + ZF, zr.at[k, 0])
         for ab, way in ((0, -1), (1, 1)):
-            arrived(b + ZF + ab, zr.at[k, 0, ab])
             zc[k, ab] = (zf[k, ab, 0] + zr[k, 0, ab].astype(f32)).astype(bf16)
             send(b + ZC + ab, zc.at[k, ab], zr.at[k, 2, ab], to("zh", way))
 
     def s5(k):
         b = k * PER
-        for ab in (0, 1):
-            arrived(b + ZD + ab, zr.at[k, 1, ab])
-        for ab in (0, 1):
-            arrived(b + ZC + ab, zr.at[k, 2, ab])
+        arrived(b + ZD, zr.at[k, 1:3])
         cols = columns(k)
         for ab in (0, 1):
             half = slice(ab * H, (ab + 1) * H)
@@ -287,8 +298,7 @@
 
     def s7(k):
         b = k * PER
-        for slot in range(7):
-            arrived(b + YS + slot, yr.at[k, slot])
+        arrived(b + YS, yr.at[k])
         total = pf[k, c, mine, :]
         for slot in range(7):
             total = total + yr[k, slot].astype(f32)
@@ -298,8 +308,7 @@
 
     def s8(k):
         b = k * PER
-        for o in (1, 2, 3):
-            arrived(b + LS + o - 1, zlb.at[k, at("zl", -o)])
+        arrived(b + LS, zlb.at[k, 0:3])
         parts = [zlb[k, n].astype(f32) for n in range(4)]
         averaged = ((parts[0] + parts[1]) + (parts[2] + parts[3])) / 32.0
         cols = columns(k)
@@ -316,8 +325,7 @@
 
     def s9(k):
         b = k * PER
-        for o in (1, 2, 3):
-            arrived(b + HS + o - 1, wbuf.at[k, x, at("zh", -o), mine_of_block, :])
+        arrived(b + HS, wbuf.at[k, x, 0:3, mine_of_block, :])
         for o in (2, 1, 3):
             piece = wbuf.at[k, x, :, mine_of_block, :]
             send(b + WY + o - 1, piece, piece, to("y", o))
@@ -327,9 +335,7 @@
 
     def s10(k):
         b = k * PER
-        for o in (1, 2, 3):
-            theirs = rows_of(c * H + at("y", -o) * Q, Q)
-            arrived(b + WY + o - 1, wbuf.at[k, x, :, theirs, :])
+        arrived(b + WY, wbuf.at[k, x, 0:3, my_half, :])
         first, second = half_block(k, x, slice(0, 2)), half_block(k, x, slice(2, 4))
         send(b + WX, first, first, to("x", 1))
         send(b + WX + 1, second, second, to("x", -1))
@@ -350,8 +356,7 @@
     def v11(k):
         b = k * PER
         before, after = at("x", -1), at("x", 1)
-        arrived(b + WX + 2, half_block(k, before, slice(2, 4)))
-        arrived(b + WX + 3, half_block(k, after, slice(0, 2)))
+        arrived(b + WX + 2, half_block(k, before))
         for n, at_x in ((1, before), (2, after)):
             block = half_block(k, at_x)
             send(b + WC + n, block, block, partner)
@@ -359,8 +364,7 @@
     def s12(k):
         b = k * PER
         far = at("x", 2)
-        arrived(b + WF, half_block(k, far, slice(0, 2)))
-        arrived(b + WF + 1, half_block(k, far, slice(2, 4)))
+        arrived(b + WF, half_block(k, far))
         block = half_block(k, far)
         send(b + WC + 3, block, block, partner)
 
@@ -397,9 +401,7 @@
 
     def t1(k):
         b = k * PER
-        for o in (1, 2, 3):
-            theirs = rows_of(c * H + at("y", -o) * Q, Q)
-            arrived(b + AY + o - 1, avgt.at[k, theirs, :])
+        arrived(b + AY, avgt.at[k, 0:3 * Q, :])
         piece = avgt.at[k, my_half, :]
         send(b + AC, piece, piece, partner)
 
@@ -419,15 +421,13 @@
             send(CX + o - 1, cmx.at[x], cmx.at[x], to("x", o))
 
     def u1():
-        for o in (1, 2, 3):
-            arrived(CX + o - 1, cmx.at[at("x", -o)])
+        arrived(CX, cmx.at[0:3])
         cmz[zh] = jnp.maximum(jnp.maximum(cmx[0], cmx[1]), jnp.maximum(cmx[2], cmx[3]))
         for o in (1, 2, 3):
             send(CZ + o - 1, cmz.at[zh], cmz.at[zh], to("zh", o))
 
     def u2():
-        for o in (1, 2, 3):
-            arrived(CZ + o - 1, cmz.at[at("zh", -o)])
+        arrived(CZ, cmz.at[0:3])
         cols_max = jnp.maximum(jnp.maximum(cmz[0], cmz[1]), jnp.maximum(cmz[2], cmz[3])) + stat_eps
         fcm_o[...] = cols_max[0:1]
         scm_o[...] = cols_max[1:2]
@@ -458,7 +458,7 @@
         name, *chunk = entry.split(":")
         with jax.named_scope("_".join([name, *chunk])):
             stages[name](*map(int, chunk))
-    for copy in started:
+    for copy in started[-NSEND:]:
         copy.wait_send()
     for copy in leaving:
         copy.wait()
@@ -496,9 +496,9 @@
         out_specs=(hbm,) * 9,
         scratch_shapes=[
             *(pltpu.VMEM(a.shape, a.dtype) for a in arguments),
-            pltpu.SemaphoreType.DMA((24,)),
+            pltpu.SemaphoreType.DMA((12,)),
             *(pltpu.VMEM(a.shape, a.dtype) for a in outs),
-            pltpu.SemaphoreType.DMA((16,)),
+            pltpu.SemaphoreType.DMA((11,)),
             pltpu.VMEM((NC, 4, 2, 4, H, T), bf16),
             pltpu.VMEM((NC, 3, 2, 4, H, T), bf16),
             pltpu.VMEM((NC, 2, 4, H, T), bf16),
@@ -520,8 +520,8 @@
             pltpu.VMEM((4, 2, 768), f32),
             pltpu.VMEM((T, 768), f32),
             pltpu.VMEM((T, 768), f32),
-            pltpu.SemaphoreType.DMA((NSEM,)),
-            pltpu.SemaphoreType.DMA((NSEM,)),
+            pltpu.SemaphoreType.DMA((NSEND,)),
+            pltpu.SemaphoreType.DMA((NRECV,)),
         ],
         compiler_params=pltpu.CompilerParams(
             collective_id=0, has_side_effects=True, vmem_limit_bytes=67043328

time: 86.5 us -> 82.8 us (0.957)
  Pallas kernels: 85.7 us -> 82 us
    pallas_call x1, Pallas kernels: 83.2 us -> 79.4 us  [local(): pl.pallas_call(kernel, out_shape=outs, in_specs=[hbm] * 9, out_specs=(hbm...]
where the time goes in v5:
time: 82.8 us; the launch traced here: 82.6 us
  Pallas kernels  82 us (99%)
    pallas_call x1, Pallas kernels, local(): pl.pallas_call(kernel, out_shape=outs, in_specs=[hbm] * 9, out_specs=(hbm...  79.4 us
    pallas_call x1, Pallas kernels, local(): pl.pallas_call(deliver, out_shape=outs, in_specs=[hbm] * 9, out_specs=(hb...  2.56 us

profile of v5, /device:TPU:1, one launch (start us, length us, event | category | flops | bytes accessed | tf_op | source)
XLA Modules:
  0.0 82.6 jit_solution(14744458852033262580)
XLA Ops:
  0.6 79.4 %round.1 = (f32[128,768]{1,0:T(8,128)}, f32[128,768]{1,0:T(8,128)}, bf16[1,128,768]{2,1,0:T(8,128)(2,1)}, bf16[1,128,768]{2,1,0:T(8,128)(2,1)}, f32[1,128]{1,0:T...) custom-call(bf16[1,512,2048]{2,1,0:T(8,128)(2,1)} %tok_h.1, ...), custom_call_target="tpu_custom_call" | custom-call | tf_op jit(solution)/shard_map/round/pallas_call | solution.py:492
  80.1 2.6 %deliver.1 = (f32[128,768]{1,0:T(8,128)}, f32[128,768]{1,0:T(8,128)}, bf16[1,128,768]{2,1,0:T(8,128)(2,1)}, bf16[1,128,768]{2,1,0:T(8,128)(2,1)}, f32[1,128]{1,0...) custom-call(f32[128,768]{1,0:T(8,128)} %get-tuple-element.18.refs_0_, ...), custom_call_target="tpu_custom_call" | custom-call | tf_op jit(solution)/shard_map/deliver/pallas_call | solution.py:531

commit v6 on v5

--- a/solution.py
+++ b/solution.py
@@ -39,7 +39,7 @@
 )
 PER_SEM = 20
 NRECV = NC * PER_SEM + 2
-NSEND = 64
+NSEND = 32
 
 
 def receive_semaphore(number):
@@ -466,8 +466,16 @@
 
 def deliver(*refs):
     sources, targets, held, arrive, depart = refs[:9], refs[9:18], refs[18:27], refs[27], refs[28]
-    inward = [pltpu.make_async_copy(src, mid, arrive.at[n]) for n, (src, mid) in enumerate(zip(sources, held))]
-    outward = [pltpu.make_async_copy(mid, dst, depart.at[n]) for n, (mid, dst) in enumerate(zip(held, targets))]
+    moves = []
+    for src, mid, dst in zip(sources, held, targets):
+        if len(src.shape) == 3 and src.shape[1] > 128:
+            for n in range(4):
+                part = slice(n * 128, (n + 1) * 128)
+                moves.insert(n, (src.at[:, part], mid.at[:, part], dst.at[:, part]))
+        else:
+            moves.append((src, mid, dst))
+    inward = [pltpu.make_async_copy(src, mid, arrive.at[n]) for n, (src, mid, _) in enumerate(moves)]
+    outward = [pltpu.make_async_copy(mid, dst, depart.at[n]) for n, (_, mid, dst) in enumerate(moves)]
     for copy in inward:
         copy.start()
     for into, out in zip(inward, outward):
@@ -535,8 +543,8 @@
         out_specs=(hbm,) * 9,
         scratch_shapes=[
             *(pltpu.VMEM(a.shape, a.dtype) for a in outs),
-            pltpu.SemaphoreType.DMA((9,)),
-            pltpu.SemaphoreType.DMA((9,)),
+            pltpu.SemaphoreType.DMA((12,)),
+            pltpu.SemaphoreType.DMA((12,)),
         ],
         compiler_params=pltpu.CompilerParams(vmem_limit_bytes=67043328),
         name="deliver",

time: 82.8 us -> 82.4 us (level)
  no operation moved by 1% of the time
where the time goes in v6:
time: 82.4 us; the launch traced here: 82.2 us
  Pallas kernels  81.6 us (99%)
    pallas_call x1, Pallas kernels, local(): pl.pallas_call(kernel, out_shape=outs, in_specs=[hbm] * 9, out_specs=(hbm...  79 us
    pallas_call x1, Pallas kernels, local(): pl.pallas_call(deliver, out_shape=outs, in_specs=[hbm] * 9, out_specs=(hb...  2.58 us

profile of v6, /device:TPU:1, one launch (start us, length us, event | category | flops | bytes accessed | tf_op | source)
XLA Modules:
  0.0 82.2 jit_solution(4949498335057253822)
XLA Ops:
  0.6 79.0 %round.1 = (f32[128,768]{1,0:T(8,128)}, f32[128,768]{1,0:T(8,128)}, bf16[1,128,768]{2,1,0:T(8,128)(2,1)}, bf16[1,128,768]{2,1,0:T(8,128)(2,1)}, f32[1,128]{1,0:T...) custom-call(bf16[1,512,2048]{2,1,0:T(8,128)(2,1)} %tok_h.1, ...), custom_call_target="tpu_custom_call" | custom-call | tf_op jit(solution)/shard_map/round/pallas_call | solution.py:500
  79.7 2.6 %deliver.1 = (f32[128,768]{1,0:T(8,128)}, f32[128,768]{1,0:T(8,128)}, bf16[1,128,768]{2,1,0:T(8,128)(2,1)}, bf16[1,128,768]{2,1,0:T(8,128)(2,1)}, f32[1,128]{1,0...) custom-call(f32[128,768]{1,0:T(8,128)} %get-tuple-element.18.refs_0_, ...), custom_call_target="tpu_custom_call" | custom-call | tf_op jit(solution)/shard_map/deliver/pallas_call | solution.py:539
